TPU v7x, 512 devices: a whole 4x8x8 slice. The times are simulated.
512 devices in a mesh: gx: 8 (over x, core), gy: 8 (over y), gz: 8 (over z).
Axes of the slice: x: 4, y: 8, z: 8, core: 2. Of those that a mesh axis runs over, the one named last changes fastest.
Arguments:
- warped_image: float32 [512, 512, 1024], P('gx', 'gy', 'gz'), may hold values from -6 to 6
- fixed_image: float32 [512, 512, 1024], P('gx', 'gy', 'gz'), may hold values from -6 to 6
- fine_control: float32 [3, 64, 64, 128], P(None, 'gx', 'gy', 'gz'), may hold values from -6 to 6
- coarse_control: float32 [3, 16, 16, 32], replicated, may hold values from -6 to 6
Outputs:
- fine_gradient: float32 [3, 64, 64, 128], P(None, 'gx', 'gy', 'gz')
- coarse_gradient: float32 [3, 16, 16, 32], replicated
All inputs are finite; a program needn't handle non-finite values.
Results may differ from a plain program's by a relative error of at most 0.0003.
Values sent between devices are 32-bit elements; how exact they have to be, the bound alone decides.
A program may use at most 64 MiB of HBM per device.

v0:
```python
import functools

import jax
import jax.numpy as jnp
from jax import lax
from jax.experimental import pallas as pl
from jax.experimental.pallas import tpu as pltpu
from jax.sharding import PartitionSpec as P

SPF = 8
SPC = 32
BEND = 0.01
HI = lax.Precision.HIGHEST
MESH = pl.DeviceIdType.MESH
f32 = jnp.float32
bf16 = jnp.bfloat16


def nn(a, b):
    return lax.dot_general(
        a, b, (((1,), (0,)), ((), ())), precision=HI, preferred_element_type=f32
    )


def nt(a, b):
    return lax.dot_general(
        a, b, (((1,), (1,)), ((), ())), precision=HI, preferred_element_type=f32
    )


def spline(t):
    m = jnp.abs(t)
    inner = 2.0 / 3.0 - m * m + 0.5 * m * m * m
    r = 2.0 - m
    outer = r * r * r * (1.0 / 6.0)
    return jnp.where(m < 1.0, inner, jnp.where(m < 2.0, outer, 0.0))


def weight(voxel, point, spacing):
    scaled = (2 * voxel + 1 - spacing * (2 * point + 1)).astype(f32)
    return spline(scaled * (0.5 / spacing))


def iota(shape, axis):
    return lax.broadcasted_iota(jnp.int32, shape, axis)


def diff1(out, inp):
    d = jnp.abs(out - inp)
    return jnp.where(d == 0, -2.0, jnp.where(d == 1, 1.0, 0.0)).astype(f32)


def diff2(out, inp, count):
    d = jnp.abs(out - inp)
    edge = (inp == 0) | (inp == count - 1)
    centre = jnp.where(edge, 5.0, 6.0)
    return jnp.where(
        d == 0, centre, jnp.where(d == 1, -4.0, jnp.where(d == 2, 1.0, 0.0))
    ).astype(f32)


def same(out, inp):
    return jnp.where(out == inp, 1.0, 0.0).astype(f32)


def bend_planes(px, py, qx, qy, cx, cy):
    jx, jy = same(px, qx), same(py, qy)
    tx, ty = diff1(px, qx), diff1(py, qy)
    m0 = diff2(px, qx, cx) * jy + jx * diff2(py, qy, cy) + 2.0 * tx * ty
    m1 = 2.0 * (tx * jy + jx * ty)
    return m0 * BEND, m1 * BEND, jx * jy * BEND


def kernel(sizes, w_hbm, f_hbm, fc_hbm, cc_hbm, fo_ref, co_ref,
           w_v, f_v, fc_ref, cc_ref, s_v, ysend, yrecv, zsend, zrecv, zcorr,
           wf_v, wc_v, fh_v, fl_v,
           accf, accc, tz_v, bend_v, ccp, bendc, zmsg, zgot, a_v, agot, b_v, bgot,
           cslots, load_sem, small_sem, hs_sem, hr_sem, ys_sem, yr_sem,
           ms_sem, mr_sem, cs_sem, cr_sem):
    nx, ny, nz = sizes
    axes = ("gx", "gy", "gz")
    counts = sizes
    me = [lax.axis_index(a) for a in axes]
    SX, SY, SZ = w_v.shape
    PX, PY, PZ = SX // SPF, SY // SPF, SZ // SPF
    KX, KY, KZ = cc_ref.shape[1:]
    EX, QE, QC = PX + 4, 2 * PY, accc.shape[1]
    cells = SX // SPF
    lanes = 3 * SZ

    loads = []
    for c in range(cells):
        part = pl.ds(c * SPF, SPF)
        loads.append((
            pltpu.make_async_copy(w_hbm.at[part], w_v.at[part], load_sem.at[0, c]),
            pltpu.make_async_copy(f_hbm.at[part], f_v.at[part], load_sem.at[1, c]),
        ))
    small = (pltpu.make_async_copy(fc_hbm, fc_ref, small_sem.at[0]),
             pltpu.make_async_copy(cc_hbm, cc_ref, small_sem.at[1]))
    order = [0, cells - 1] + list(range(1, cells - 1))
    for c in order:
        loads[c][0].start()
        loads[c][1].start()
    for copy in small:
        copy.start()

    zero_plane = jnp.zeros((2, SY, SZ), f32)
    s_v[0:2, 8:8 + SY, :] = zero_plane
    s_v[SX + 2:SX + 4, 8:8 + SY, :] = zero_plane
    yrecv[...] = jnp.zeros(yrecv.shape, f32)
    zrecv[...] = jnp.zeros(zrecv.shape, f32)
    zgot[...] = jnp.zeros(zgot.shape, f32)
    agot[...] = jnp.zeros(agot.shape, f32)
    bgot[...] = jnp.zeros(bgot.shape, f32)

    barrier = pltpu.get_barrier_semaphore()
    total = 0
    for k, a in enumerate(axes):
        for d in range(1, counts[k]):
            pl.semaphore_signal(
                barrier, inc=1, device_id={a: lax.rem(me[k] + d, counts[k])}, device_id_type=MESH
            )
            total += 1

    def split_store(ref, index, value):
        high = value.astype(bf16)
        ref[index + (0,)] = high
        ref[index + (1,)] = (value - high.astype(f32)).astype(bf16)

    KC = SPF * SY
    def ext_q(q):
        return jnp.where(q < PY, q, jnp.where(q < PY + 2, q - PY - 2, q - 2))

    rows, cols = iota((5 * QE, KC), 0), iota((5 * QE, KC), 1)
    split_store(wf_v, (), weight(cols // SY, rows // QE - 2, SPF)
                * weight(cols % SY, ext_q(rows % QE), SPF))
    rows, cols = iota((4 * QC, KC), 0), iota((4 * QC, KC), 1)
    along_y = weight(cols % SY + me[1] * SY, rows % QC, SPC)
    for ph in range(SPC // SPF):
        first = -2 if ph < SPC // SPF // 2 else -1
        split_store(wc_v, (ph,),
                    weight(cols // SY + ph * SPF, rows // QC + first, SPC) * along_y)

    pl.semaphore_wait(barrier, total)

    has = [(me[k] > 0, me[k] < counts[k] - 1) for k in range(3)]
    pieces = ys_sem.shape[1]
    each = SX // pieces

    def halo(k, side, piece=0):
        if k == 1:
            part = pl.ds(piece * each, each)
            return neighbour_copy(
                k, side, ysend.at[side, part], yrecv.at[1 - side, part],
                ys_sem.at[side, piece], yr_sem.at[1 - side, piece])
        if k == 0:
            src = s_v.at[pl.ds(2 if side == 0 else SX, 2), pl.ds(8, SY), :]
            dst = s_v.at[pl.ds(SX + 2 if side == 0 else 0, 2), pl.ds(8, SY), :]
        else:
            src, dst = zsend.at[side], zrecv.at[1 - side]
        return neighbour_copy(k, side, src, dst, hs_sem.at[k, side], hr_sem.at[k, 1 - side])

    def neighbour_copy(k, side, src, dst, send, recv):
        other = me[k] - 1 if side == 0 else me[k] + 1
        return pltpu.make_async_remote_copy(
            src_ref=src, dst_ref=dst, send_sem=send, recv_sem=recv,
            device_id={axes[k]: other}, device_id_type=MESH,
        )

    def start_halo(k, side, piece=0):
        @pl.when(has[k][side])
        def _():
            halo(k, side, piece).start()

    lane = iota((SY, SZ), 1)

    def one_slab(x, carry):
        low, high = carry
        s = w_v[x] + f_v[x]
        s_v[x + 2, 8:8 + SY, :] = s
        ysend[0, x] = s[0:2]
        ysend[1, x] = s[SY - 2:SY]
        here = lane // 2 == x
        low = jnp.where(here, pltpu.roll(s, 2 * x, 1), low)
        high = jnp.where(here, pltpu.roll(s, lax.rem(2 * x + 2, SZ), 1), high)
        return low, high

    carry = (jnp.zeros((SY, SZ), f32), jnp.zeros((SY, SZ), f32))
    done = set()
    sent = set()
    for c in order:
        for copy in loads[c]:
            copy.wait()
        carry = lax.fori_loop(c * SPF, (c + 1) * SPF, one_slab, carry)
        done.add(c)
        for piece in range(pieces):
            inside = range(piece * each // SPF, (piece + 1) * each // SPF)
            if piece not in sent and all(n in done for n in inside):
                sent.add(piece)
                start_halo(1, 0, piece)
                start_halo(1, 1, piece)
        if c == 0:
            start_halo(0, 0)
        if c == cells - 1:
            start_halo(0, 1)
    zsend[0] = carry[0]
    zsend[1] = carry[1]
    start_halo(2, 0)
    start_halo(2, 1)

    accf[...] = jnp.zeros(accf.shape, f32)
    accc[...] = jnp.zeros(accc.shape, f32)
    for copy in small:
        copy.wait()
    shape = (EX * QE, PX * PY)
    rows, cols = iota(shape, 0), iota(shape, 1)
    ox, oy = me[0] * PX, me[1] * PY
    outer, inner = rows // (EX * PY), rows % (EX * PY)
    planes = bend_planes(inner // PY - 2 + ox, ext_q(inner % PY + PY * outer) + oy,
                         cols // PY + ox, cols % PY + oy, PX * nx, PY * ny)
    RZ = tz_v.shape[2]

    def ext_point(row):
        return jnp.where(row < PZ, row, jnp.where(row < PZ + 2, row - PZ - 2, row - 2))

    oz = me[2] * PZ
    zr, zc = ext_point(iota((RZ, PZ), 0)) + oz, iota((RZ, PZ), 1) + oz
    along = (same(zr, zc), diff1(zr, zc), diff2(zr, zc, PZ * nz))
    for a in range(3):
        block = fc_ref[a].reshape(PX * PY, PZ)
        factors = [nn(plane, block) for plane in planes]
        for half in range(2):
            part = slice(half * EX * PY, (half + 1) * EX * PY)
            bend_v[half, a] = (nt(along[0], factors[0][part]) + nt(along[1], factors[1][part])
                               + nt(along[2], factors[2][part]))
    shape = (KX * QC, KX * QC)
    rows, cols = iota(shape, 0), iota(shape, 1)
    planes = bend_planes(rows // QC, rows % QC, cols // QC, cols % QC, KX, KY)
    zr, zc = iota((KZ, KZ), 0), iota((KZ, KZ), 1)
    for a in range(3):
        for p in range(KX):
            ccp[a, p * QC:p * QC + KY, :] = cc_ref[a, p]
        block = ccp[a]
        bendc[a] = (nn(planes[0], block) + nn(planes[1], nn(block, diff1(zr, zc)))
                    + BEND * nn(block, diff2(zr, zc, KZ)))

    for k in (0, 1, 2):
        for side in range(2):
            for piece in range(pieces if k == 1 else 1):
                @pl.when(has[k][side])
                def _(k=k, side=side, piece=piece):
                    halo(k, side, piece).wait_send()

                @pl.when(has[k][1 - side])
                def _(k=k, side=side, piece=piece):
                    halo(k, side, piece).wait_recv()

    even = lane % 2 == 0
    dl = zrecv[0] - zsend[1]
    dh = zrecv[1] - zsend[0]
    zcorr[0] = jnp.where(even, dl - 8.0 * pltpu.roll(dl, SZ - 1, 1), dl)
    zcorr[1] = jnp.where(even, -dh, 8.0 * pltpu.roll(dh, 1, 1) - dh)

    def forces(i):
        slot = i % 2
        for xx in range(SPF):
            x = i * SPF + xx
            s_v[x + 2, 6:8, :] = yrecv[0, x]
            s_v[x + 2, 8 + SY:10 + SY, :] = yrecv[1, x]
            d = w_v[x] - f_v[x]
            s = s_v[x + 2, 8:8 + SY, :]
            gx = (s_v[x, 8:8 + SY, :] - s_v[x + 4, 8:8 + SY, :]
                  + 8.0 * (s_v[x + 3, 8:8 + SY, :] - s_v[x + 1, 8:8 + SY, :]))
            gy = (s_v[x + 2, 6:6 + SY, :] - s_v[x + 2, 10:10 + SY, :]
                  + 8.0 * (s_v[x + 2, 9:9 + SY, :] - s_v[x + 2, 7:7 + SY, :]))
            gz = (pltpu.roll(s, 2, 1) - pltpu.roll(s, SZ - 2, 1)
                  + 8.0 * (pltpu.roll(s, SZ - 1, 1) - pltpu.roll(s, 1, 1)))
            corr = jnp.where(lane < 2, pltpu.roll(zcorr[0], (SZ - 2 * x) % SZ, 1), 0.0)
            corr = jnp.where(lane >= SZ - 2,
                             pltpu.roll(zcorr[1], (2 * SZ - 2 - 2 * x) % SZ, 1), corr)
            gz = gz + corr
            for a, g in enumerate((gx, gy, gz)):
                force = g * d
                high = force.astype(bf16)
                fh_v[slot, xx * SY:(xx + 1) * SY, a * SZ:(a + 1) * SZ] = high
                fl_v[slot, xx * SY:(xx + 1) * SY, a * SZ:(a + 1) * SZ] = (
                    force - high.astype(f32)).astype(bf16)

    def gather(i):
        slot = i % 2
        k, ph = divmod(i, SPC // SPF)
        many = 5 * QE + 4 * QC
        weights = jnp.concatenate([wf_v[0], wc_v[ph, 0], wf_v[1], wc_v[ph, 1]], axis=0)
        both = jnp.dot(weights, fh_v[slot], preferred_element_type=f32)
        out = both[:many] + both[many:] + jnp.dot(
            weights[:many], fl_v[slot], preferred_element_type=f32)
        fine = out[:5 * QE].reshape(5, 2, PY, lanes)
        accf[0, i:i + 5] += fine[:, 0]
        accf[1, i:i + 5] += fine[:, 1]
        at = me[0] * (SX // SPC) + k + (1 if ph >= SPC // SPF // 2 else 0)
        accc[pl.ds(at, 4)] += out[5 * QE:].reshape(4, QC, lanes)

    forces(0)
    for i in range(cells):
        if i + 1 < cells:
            forces(i + 1)
        gather(i)

    rows, cols = iota((RZ, SZ), 0), iota((RZ, SZ), 1)
    bz = weight(cols, ext_point(rows), SPF) * (SPF ** -1.5 / 24.0)
    rows, cols = iota((KZ, SZ), 0), iota((KZ, SZ), 1)
    bzc = weight(cols + me[2] * SZ, rows, SPC) * (SPC ** -1.5 / 24.0)
    for a in range(3):
        for half in range(2):
            block = accf[half, :, :, a * SZ:(a + 1) * SZ].reshape(EX * PY, SZ)
            tz_v[half, a] = nt(bz, block) + bend_v[half, a]
            for side in range(2):
                zmsg[side, half, 2 * a:2 * a + 2, :] = tz_v[
                    half, a, PZ + 2 * side:PZ + 2 * side + 2, :]
    blocks = [accc[2:2 + KX, :, a * SZ:(a + 1) * SZ].reshape(KX * QC, SZ) for a in range(3)]
    cslots[2, me[2]] = nt(bzc, jnp.concatenate(blocks, axis=0))

    def coarse_copy(k, d, slot):
        n = counts[k]
        return pltpu.make_async_remote_copy(
            src_ref=cslots.at[k, slot], dst_ref=cslots.at[k, slot],
            send_sem=cs_sem.at[k, d], recv_sem=cr_sem.at[k, d],
            device_id={axes[k]: lax.rem(me[k] + d, n)}, device_id_type=MESH,
        )

    def exchange(k, source, got):
        for side in range(2):
            @pl.when(has[k][side])
            def _(side=side):
                neighbour_copy(k, side, source(side), got.at[1 - side],
                               ms_sem.at[k, side], mr_sem.at[k, 1 - side]).start()
        for d in range(1, counts[k]):
            coarse_copy(k, d, me[k]).start()
        for side in range(2):
            @pl.when(has[k][side])
            def _(side=side):
                neighbour_copy(k, side, source(side), got.at[1 - side],
                               ms_sem.at[k, side], mr_sem.at[k, 1 - side]).wait_send()

            @pl.when(has[k][1 - side])
            def _(side=side):
                neighbour_copy(k, side, source(side), got.at[1 - side],
                               ms_sem.at[k, side], mr_sem.at[k, 1 - side]).wait_recv()
        for d in range(1, counts[k]):
            coarse_copy(k, d, me[k]).wait_send()
            coarse_copy(k, d, lax.rem(me[k] + counts[k] - d, counts[k])).wait_recv()
        whole = cslots[k, 0]
        for n in range(1, counts[k]):
            whole = whole + cslots[k, n]
        return whole

    whole = exchange(2, lambda side: zmsg.at[side], zgot)
    for half in range(2):
        for a in range(3):
            tz_v[half, a, 0:2, :] = tz_v[half, a, 0:2, :] + zgot[0, half, 2 * a:2 * a + 2, :]
            tz_v[half, a, PZ - 2:PZ, :] = (
                tz_v[half, a, PZ - 2:PZ, :] + zgot[1, half, 2 * a:2 * a + 2, :])
            a_v[half, a * PZ:(a + 1) * PZ, :] = tz_v[half, a, 0:PZ, :]

    cslots[1, me[1]] = whole
    whole = exchange(1, lambda side: a_v.at[1], agot)
    shape = (EX * PY, EX * PY)
    rows, cols = iota(shape, 0), iota(shape, 1)
    p_same = rows // PY == cols // PY
    q, r = rows % PY, cols % PY
    low = jnp.where(p_same & (q == r + 2) & (r < 2), 1.0, 0.0)
    high = jnp.where(p_same & (q == r - (PY - 2)) & (r >= PY - 2), 1.0, 0.0)
    b_v[...] = a_v[0] + nn(agot[0], low) + nn(agot[1], high)

    cslots[0, me[0]] = whole
    whole = exchange(0, lambda side: b_v, bgot)
    shape = (PX * PY, EX * PY)
    rows, cols = iota(shape, 0), iota(shape, 1)
    own = jnp.where(cols == rows + 2 * PY, 1.0, 0.0)
    low = jnp.where((cols == rows + (PX + 2) * PY) & (rows < 2 * PY), 1.0, 0.0)
    high = jnp.where((cols == rows - (PX - 2) * PY) & (rows >= (PX - 2) * PY), 1.0, 0.0)
    shape = (3 * KX * QC, 3 * KX * QC)
    turned = nt(same(iota(shape, 0), iota(shape, 1)), whole)
    for a in range(3):
        part = slice(a * PZ, (a + 1) * PZ)
        out = nt(own, b_v[part]) + nt(low, bgot[0, part]) + nt(high, bgot[1, part])
        fo_ref[a] = out.reshape(PX, PY, PZ)
        out = turned[a * KX * QC:(a + 1) * KX * QC] + bendc[a]
        for p in range(KX):
            co_ref[a, p] = out[p * QC:p * QC + KY, :]


def solution(mesh):
    sizes = tuple(mesh.shape[a] for a in ("gx", "gy", "gz"))

    def step(warped, fixed, fine, coarse):
        SX, SY, SZ = warped.shape
        PX, PY, PZ = SX // SPF, SY // SPF, SZ // SPF
        KX, KY, KZ = coarse.shape[1:]
        QC = KY
        EX, QE, RZ = PX + 4, 2 * PY, PZ + 8
        KC = SPF * SY
        most = max(sizes)
        vmem = pl.BlockSpec(memory_space=pltpu.VMEM)
        hbm = pl.BlockSpec(memory_space=pltpu.HBM)
        V = pltpu.VMEM
        D = pltpu.SemaphoreType.DMA
        return pl.pallas_call(
            functools.partial(kernel, sizes),
            out_shape=(jax.ShapeDtypeStruct(fine.shape, f32),
                       jax.ShapeDtypeStruct(coarse.shape, f32)),
            in_specs=[hbm] * 4,
            out_specs=(vmem, vmem),
            scratch_shapes=[
                V((SX, SY, SZ), f32), V((SX, SY, SZ), f32),
                V((3, PX, PY, PZ), f32), V(coarse.shape, f32),
                V((SX + 4, SY + 16, SZ), f32),
                V((2, SX, 2, SZ), f32), V((2, SX, 2, SZ), f32),
                V((2, SY, SZ), f32), V((2, SY, SZ), f32), V((2, SY, SZ), f32),
                V((2, 5 * QE, KC), bf16), V((SPC // SPF, 2, 4 * QC, KC), bf16),
                V((2, KC, 3 * SZ), bf16), V((2, KC, 3 * SZ), bf16),
                V((2, EX, PY, 3 * SZ), f32), V((KX + 4, QC, 3 * SZ), f32),
                V((2, 3, RZ, EX * PY), f32), V((2, 3, RZ, EX * PY), f32),
                V((3, KX * QC, KZ), f32), V((3, KX * QC, KZ), f32),
                V((2, 2, 8, EX * PY), f32), V((2, 2, 8, EX * PY), f32),
                V((2, 3 * PZ, EX * PY), f32), V((2, 3 * PZ, EX * PY), f32),
                V((3 * PZ, EX * PY), f32), V((2, 3 * PZ, EX * PY), f32),
                V((3, most, KZ, 3 * KX * QC), f32),
                D((2, SX // SPF)), D((2,)), D((3, 2)), D((3, 2)), D((2, 4)), D((2, 4)),
                D((3, 2)), D((3, 2)), D((3, most)), D((3, most)),
            ],
            compiler_params=pltpu.CompilerParams(
                collective_id=0, has_side_effects=True, vmem_limit_bytes=66000000
            ),
        )(warped, fixed, fine, coarse)

    in_specs = (P("gx", "gy", "gz"), P("gx", "gy", "gz"), P(None, "gx", "gy", "gz"), P())
    out_specs = (P(None, "gx", "gy", "gz"), P())
    return jax.shard_map(
        step, mesh=mesh, in_specs=in_specs, out_specs=out_specs, check_vma=False
    )
```

profile of v0, /device:TPU:1, one launch (start us, length us, event | category | flops | bytes accessed | tf_op | source)
XLA Modules:
  0.0 87.0 jit_solution(3402746603978082010)
XLA Ops:
  0.6 83.1 %shard_map.59 = (f32[3,8,8,16]{3,2,1,0:T(8,128)}, f32[3,16,16,32]{3,2,1,0:T(8,128)}) custom-call(f32[64,64,128]{2,1,0:T(8,128)} %w_hbm.1, f32[64,64,128]{2,1,0:T(8,128)} %f_hbm.1, f32[3,8,8,16]{3,2,1,0:T(8,128)} %fc_hbm.1, f32[3,16,16,32]{3,2,1,0:T(8,128)} %cc_hbm.1), custom_call_target="tpu_custom_call" | custom-call | tf_op jit(solution)/shard_map/pallas_call | solution.py:408
  83.7 1.5 %copy.8 = f32[3,8,8,16]{3,2,1,0:T(8,128)} copy(f32[3,8,8,16]{3,2,1,0:T(8,128)} %get-tuple-element.4) | data formatting | bytes 24576
  85.3 1.8 %copy.9 = f32[3,16,16,32]{3,2,1,0:T(8,128)} copy(f32[3,16,16,32]{3,2,1,0:T(8,128)} %get-tuple-element.5) | data formatting | bytes 196608
where the time goes:
time: 87.9 us; the launch traced here: 87 us
  Pallas kernels  83.1 us (95%)
  local copies, waits for them, and re-layouts  3.31 us (4%)
    pallas_call x1, Pallas kernels, step(): pl.pallas_call(functools.partial(kernel, sizes), out_shape=(jax.ShapeDtyp...  83.1 us
    unnamed x2, local copies, waits for them, and re-layouts  3.31 us

commit v1 on v0

--- a/solution.py
+++ b/solution.py
@@ -74,9 +74,9 @@
 def kernel(sizes, w_hbm, f_hbm, fc_hbm, cc_hbm, fo_ref, co_ref,
            w_v, f_v, fc_ref, cc_ref, s_v, ysend, yrecv, zsend, zrecv, zcorr,
            wf_v, wc_v, fh_v, fl_v,
-           accf, accc, tz_v, bend_v, ccp, bendc, zmsg, zgot, a_v, agot, b_v, bgot,
-           cslots, load_sem, small_sem, hs_sem, hr_sem, ys_sem, yr_sem,
-           ms_sem, mr_sem, cs_sem, cr_sem):
+           accf, accc, tz_v, bend_v, clane, cbend, zmsg, zgot, a_v, agot, b_v, bgot,
+           cmsg, crecv, zrow, xrow, load_sem, small_sem, hs_sem, hr_sem, ys_sem, yr_sem,
+           ms_sem, mr_sem, ns_sem, nr_sem, cs_sem, cr_sem):
     nx, ny, nz = sizes
     axes = ("gx", "gy", "gz")
     counts = sizes
@@ -84,7 +84,8 @@
     SX, SY, SZ = w_v.shape
     PX, PY, PZ = SX // SPF, SY // SPF, SZ // SPF
     KX, KY, KZ = cc_ref.shape[1:]
-    EX, QE, QC = PX + 4, 2 * PY, accc.shape[1]
+    EX, QE = PX + 4, 2 * PY
+    CR = accc.shape[0]
     cells = SX // SPF
     lanes = 3 * SZ
 
@@ -104,6 +105,17 @@
     for copy in small:
         copy.start()
 
+    has = [(me[k] > 0, me[k] < counts[k] - 1) for k in range(3)]
+    sides = [(d, e, f) for f in range(3) for d in range(3) for e in range(3)]
+
+    def toward(step):
+        ok = None
+        for k in range(3):
+            if step[k] != 1:
+                here = has[k][0] if step[k] == 0 else has[k][1]
+                ok = here if ok is None else ok & here
+        return ok, {axes[k]: me[k] + (step[k] - 1) for k in range(3) if step[k] != 1}
+
     zero_plane = jnp.zeros((2, SY, SZ), f32)
     s_v[0:2, 8:8 + SY, :] = zero_plane
     s_v[SX + 2:SX + 4, 8:8 + SY, :] = zero_plane
@@ -112,6 +124,7 @@
     zgot[...] = jnp.zeros(zgot.shape, f32)
     agot[...] = jnp.zeros(agot.shape, f32)
     bgot[...] = jnp.zeros(bgot.shape, f32)
+    crecv[...] = jnp.zeros(crecv.shape, f32)
 
     barrier = pltpu.get_barrier_semaphore()
     total = 0
@@ -121,6 +134,15 @@
                 barrier, inc=1, device_id={a: lax.rem(me[k] + d, counts[k])}, device_id_type=MESH
             )
             total += 1
+    for step in sides:
+        if sum(n != 1 for n in step) >= 2:
+            ok, there = toward(step)
+
+            @pl.when(ok)
+            def _(there=there):
+                pl.semaphore_signal(barrier, inc=1, device_id=there, device_id_type=MESH)
+    near = [low.astype(jnp.int32) + high.astype(jnp.int32) for low, high in has]
+    total = total + (near[0] + 1) * (near[1] + 1) * (near[2] + 1) - 1 - near[0] - near[1] - near[2]
 
     def split_store(ref, index, value):
         high = value.astype(bf16)
@@ -128,22 +150,22 @@
         ref[index + (1,)] = (value - high.astype(f32)).astype(bf16)
 
     KC = SPF * SY
+
     def ext_q(q):
         return jnp.where(q < PY, q, jnp.where(q < PY + 2, q - PY - 2, q - 2))
 
     rows, cols = iota((5 * QE, KC), 0), iota((5 * QE, KC), 1)
     split_store(wf_v, (), weight(cols // SY, rows // QE - 2, SPF)
                 * weight(cols % SY, ext_q(rows % QE), SPF))
-    rows, cols = iota((4 * QC, KC), 0), iota((4 * QC, KC), 1)
-    along_y = weight(cols % SY + me[1] * SY, rows % QC, SPC)
-    for ph in range(SPC // SPF):
-        first = -2 if ph < SPC // SPF // 2 else -1
-        split_store(wc_v, (ph,),
-                    weight(cols // SY + ph * SPF, rows // QC + first, SPC) * along_y)
+    rows, cols = iota((CR, KC), 0), iota((CR, KC), 1)
+    side, inner = rows // 4, rows % 4
+    along_y = weight(cols % SY, 2 * (side % 3) + inner % 2 - 2, SPC)
+    for c in range(cells):
+        split_store(wc_v, (c,),
+                    weight(cols // SY + c * SPF, 2 * (side // 3) + inner // 2 - 2, SPC) * along_y)
 
     pl.semaphore_wait(barrier, total)
 
-    has = [(me[k] > 0, me[k] < counts[k] - 1) for k in range(3)]
     pieces = ys_sem.shape[1]
     each = SX // pieces
 
@@ -210,47 +232,10 @@
 
     accf[...] = jnp.zeros(accf.shape, f32)
     accc[...] = jnp.zeros(accc.shape, f32)
-    for copy in small:
-        copy.wait()
-    shape = (EX * QE, PX * PY)
-    rows, cols = iota(shape, 0), iota(shape, 1)
-    ox, oy = me[0] * PX, me[1] * PY
-    outer, inner = rows // (EX * PY), rows % (EX * PY)
-    planes = bend_planes(inner // PY - 2 + ox, ext_q(inner % PY + PY * outer) + oy,
-                         cols // PY + ox, cols % PY + oy, PX * nx, PY * ny)
-    RZ = tz_v.shape[2]
-
-    def ext_point(row):
-        return jnp.where(row < PZ, row, jnp.where(row < PZ + 2, row - PZ - 2, row - 2))
-
-    oz = me[2] * PZ
-    zr, zc = ext_point(iota((RZ, PZ), 0)) + oz, iota((RZ, PZ), 1) + oz
-    along = (same(zr, zc), diff1(zr, zc), diff2(zr, zc, PZ * nz))
-    for a in range(3):
-        block = fc_ref[a].reshape(PX * PY, PZ)
-        factors = [nn(plane, block) for plane in planes]
-        for half in range(2):
-            part = slice(half * EX * PY, (half + 1) * EX * PY)
-            bend_v[half, a] = (nt(along[0], factors[0][part]) + nt(along[1], factors[1][part])
-                               + nt(along[2], factors[2][part]))
-    shape = (KX * QC, KX * QC)
-    rows, cols = iota(shape, 0), iota(shape, 1)
-    planes = bend_planes(rows // QC, rows % QC, cols // QC, cols % QC, KX, KY)
-    zr, zc = iota((KZ, KZ), 0), iota((KZ, KZ), 1)
-    for a in range(3):
-        for p in range(KX):
-            ccp[a, p * QC:p * QC + KY, :] = cc_ref[a, p]
-        block = ccp[a]
-        bendc[a] = (nn(planes[0], block) + nn(planes[1], nn(block, diff1(zr, zc)))
-                    + BEND * nn(block, diff2(zr, zc, KZ)))
 
     for k in (0, 1, 2):
         for side in range(2):
             for piece in range(pieces if k == 1 else 1):
-                @pl.when(has[k][side])
-                def _(k=k, side=side, piece=piece):
-                    halo(k, side, piece).wait_send()
-
                 @pl.when(has[k][1 - side])
                 def _(k=k, side=side, piece=piece):
                     halo(k, side, piece).wait_recv()
@@ -288,17 +273,15 @@
 
     def gather(i):
         slot = i % 2
-        k, ph = divmod(i, SPC // SPF)
-        many = 5 * QE + 4 * QC
-        weights = jnp.concatenate([wf_v[0], wc_v[ph, 0], wf_v[1], wc_v[ph, 1]], axis=0)
+        many = 5 * QE + CR
+        weights = jnp.concatenate([wf_v[0], wc_v[i, 0], wf_v[1], wc_v[i, 1]], axis=0)
         both = jnp.dot(weights, fh_v[slot], preferred_element_type=f32)
         out = both[:many] + both[many:] + jnp.dot(
             weights[:many], fl_v[slot], preferred_element_type=f32)
         fine = out[:5 * QE].reshape(5, 2, PY, lanes)
         accf[0, i:i + 5] += fine[:, 0]
         accf[1, i:i + 5] += fine[:, 1]
-        at = me[0] * (SX // SPC) + k + (1 if ph >= SPC // SPF // 2 else 0)
-        accc[pl.ds(at, 4)] += out[5 * QE:].reshape(4, QC, lanes)
+        accc[...] += out[5 * QE:]
 
     forces(0)
     for i in range(cells):
@@ -306,10 +289,67 @@
             forces(i + 1)
         gather(i)
 
+    rows, cols = iota((SZ, 128), 0), iota((SZ, 128), 1)
+    bzc = weight(rows, cols % 4 + 4 * (cols // 16 - 1), SPC) * (SPC ** -1.5 / 24.0)
+    stack = jnp.concatenate([accc[:, a * SZ:(a + 1) * SZ] for a in range(3)], axis=0)
+    shares = nn(stack, bzc)
+    rows, cols = iota((CR, 128), 0), iota((CR, 128), 1)
+    keep = (rows % 4 == (cols // 4) % 4) & (cols < 48)
+    for f in range(3):
+        value = shares[0:CR]
+        value = value if f == 0 else pltpu.roll(value, 128 - 16 * f, 1)
+        for a in (1, 2):
+            moved = shares[a * CR:(a + 1) * CR]
+            moved = moved if a == f else pltpu.roll(moved, (128 + 16 * (a - f)) % 128, 1)
+            value = jnp.where(cols // 16 == a, moved, value)
+        value = jnp.where(keep, value, 0.0).reshape(CR // 8, 8, 128)
+        value = value + pltpu.roll(value, 7, 1)
+        value = value + pltpu.roll(value, 6, 1)
+        for s in range(9):
+            row = 4 * (s % 2)
+            cmsg[f * 9 + s] = value[s // 2, row:row + 1, :]
+
+    def share_copy(n):
+        there = toward(sides[n])[1]
+        return pltpu.make_async_remote_copy(
+            src_ref=cmsg.at[n], dst_ref=crecv.at[26 - n],
+            send_sem=ns_sem.at[n], recv_sem=nr_sem.at[26 - n],
+            device_id=there, device_id_type=MESH,
+        )
+
+    far = sorted((n for n in range(27) if n != 13),
+                 key=lambda n: -sum(v != 1 for v in sides[n]))
+    for n in far:
+        @pl.when(toward(sides[n])[0])
+        def _(n=n):
+            share_copy(n).start()
+
+    for copy in small:
+        copy.wait()
+    shape = (EX * QE, PX * PY)
+    rows, cols = iota(shape, 0), iota(shape, 1)
+    ox, oy = me[0] * PX, me[1] * PY
+    outer, inner = rows // (EX * PY), rows % (EX * PY)
+    planes = bend_planes(inner // PY - 2 + ox, ext_q(inner % PY + PY * outer) + oy,
+                         cols // PY + ox, cols % PY + oy, PX * nx, PY * ny)
+    RZ = tz_v.shape[2]
+
+    def ext_point(row):
+        return jnp.where(row < PZ, row, jnp.where(row < PZ + 2, row - PZ - 2, row - 2))
+
+    oz = me[2] * PZ
+    zr, zc = ext_point(iota((RZ, PZ), 0)) + oz, iota((RZ, PZ), 1) + oz
+    along = (same(zr, zc), diff1(zr, zc), diff2(zr, zc, PZ * nz))
+    for a in range(3):
+        block = fc_ref[a].reshape(PX * PY, PZ)
+        factors = [nn(plane, block) for plane in planes]
+        for half in range(2):
+            part = slice(half * EX * PY, (half + 1) * EX * PY)
+            bend_v[half, a] = (nt(along[0], factors[0][part]) + nt(along[1], factors[1][part])
+                               + nt(along[2], factors[2][part]))
+
     rows, cols = iota((RZ, SZ), 0), iota((RZ, SZ), 1)
     bz = weight(cols, ext_point(rows), SPF) * (SPF ** -1.5 / 24.0)
-    rows, cols = iota((KZ, SZ), 0), iota((KZ, SZ), 1)
-    bzc = weight(cols + me[2] * SZ, rows, SPC) * (SPC ** -1.5 / 24.0)
     for a in range(3):
         for half in range(2):
             block = accf[half, :, :, a * SZ:(a + 1) * SZ].reshape(EX * PY, SZ)
@@ -317,53 +357,95 @@
             for side in range(2):
                 zmsg[side, half, 2 * a:2 * a + 2, :] = tz_v[
                     half, a, PZ + 2 * side:PZ + 2 * side + 2, :]
-    blocks = [accc[2:2 + KX, :, a * SZ:(a + 1) * SZ].reshape(KX * QC, SZ) for a in range(3)]
-    cslots[2, me[2]] = nt(bzc, jnp.concatenate(blocks, axis=0))
-
-    def coarse_copy(k, d, slot):
-        n = counts[k]
-        return pltpu.make_async_remote_copy(
-            src_ref=cslots.at[k, slot], dst_ref=cslots.at[k, slot],
-            send_sem=cs_sem.at[k, d], recv_sem=cr_sem.at[k, d],
-            device_id={axes[k]: lax.rem(me[k] + d, n)}, device_id_type=MESH,
-        )
-
-    def exchange(k, source, got):
+
+    def fine_copy(k, side):
+        source, got = ((b_v, bgot), (a_v.at[1], agot), (zmsg.at[side], zgot))[k]
+        return neighbour_copy(k, side, source, got.at[1 - side],
+                              ms_sem.at[k, side], mr_sem.at[k, 1 - side])
+
+    def fine_start(k):
         for side in range(2):
             @pl.when(has[k][side])
             def _(side=side):
-                neighbour_copy(k, side, source(side), got.at[1 - side],
-                               ms_sem.at[k, side], mr_sem.at[k, 1 - side]).start()
-        for d in range(1, counts[k]):
-            coarse_copy(k, d, me[k]).start()
+                fine_copy(k, side).start()
+
+    def fine_wait(k):
         for side in range(2):
-            @pl.when(has[k][side])
-            def _(side=side):
-                neighbour_copy(k, side, source(side), got.at[1 - side],
-                               ms_sem.at[k, side], mr_sem.at[k, 1 - side]).wait_send()
-
             @pl.when(has[k][1 - side])
             def _(side=side):
-                neighbour_copy(k, side, source(side), got.at[1 - side],
-                               ms_sem.at[k, side], mr_sem.at[k, 1 - side]).wait_recv()
+                fine_copy(k, side).wait_recv()
+
+    hz = nz // 2
+    slots = (xrow.at[me[0]], xrow.at[me[0], me[1]], zrow.at[me[2]])
+
+    def coarse_copy(k, d):
+        return pltpu.make_async_remote_copy(
+            src_ref=slots[k], dst_ref=slots[k],
+            send_sem=cs_sem.at[k, d], recv_sem=cr_sem.at[k, d],
+            device_id={axes[k]: lax.rem(me[k] + d, counts[k])}, device_id_type=MESH,
+        )
+
+    def coarse_from(k, d):
+        other = lax.rem(me[k] + counts[k] - d, counts[k])
+        slot = (xrow.at[other], xrow.at[me[0], other], zrow.at[other])[k]
+        return pltpu.make_async_remote_copy(
+            src_ref=slot, dst_ref=slot, send_sem=cs_sem.at[k, d], recv_sem=cr_sem.at[k, d],
+            device_id={axes[k]: other}, device_id_type=MESH,
+        )
+
+    def coarse_start(k):
+        n = counts[k]
+        for d in sorted(range(1, n), key=lambda d: -min(d, n - d)):
+            coarse_copy(k, d).start()
+
+    def coarse_wait(k):
         for d in range(1, counts[k]):
-            coarse_copy(k, d, me[k]).wait_send()
-            coarse_copy(k, d, lax.rem(me[k] + counts[k] - d, counts[k])).wait_recv()
-        whole = cslots[k, 0]
-        for n in range(1, counts[k]):
-            whole = whole + cslots[k, n]
-        return whole
-
-    whole = exchange(2, lambda side: zmsg.at[side], zgot)
+            coarse_from(k, d).wait_recv()
+
+    fine_start(2)
+
+    for n in range(27):
+        if n != 13:
+            @pl.when(toward(sides[n])[0])
+            def _(n=n):
+                share_copy(26 - n).wait_recv()
+    own = cmsg[13]
+    for n in range(27):
+        if n != 13:
+            own = own + crecv[n]
+    zrow[me[2]] = own
+    coarse_start(2)
+
+    fine_wait(2)
     for half in range(2):
         for a in range(3):
             tz_v[half, a, 0:2, :] = tz_v[half, a, 0:2, :] + zgot[0, half, 2 * a:2 * a + 2, :]
             tz_v[half, a, PZ - 2:PZ, :] = (
                 tz_v[half, a, PZ - 2:PZ, :] + zgot[1, half, 2 * a:2 * a + 2, :])
             a_v[half, a * PZ:(a + 1) * PZ, :] = tz_v[half, a, 0:PZ, :]
-
-    cslots[1, me[1]] = whole
-    whole = exchange(1, lambda side: a_v.at[1], agot)
+    fine_start(1)
+
+    q_at, r_at = iota((KX, KY, 128), 1), iota((KX, KY, 128), 2)
+
+    def laplace(c):
+        zero = jnp.zeros((1, KY, 128), f32)
+        total = (jnp.concatenate([c[1:], zero], axis=0) + jnp.concatenate([zero, c[:-1]], axis=0)
+                 + jnp.where(q_at < KY - 1, pltpu.roll(c, KY - 1, 1), 0.0)
+                 + jnp.where(q_at > 0, pltpu.roll(c, 1, 1), 0.0)
+                 + pltpu.roll(c, 127, 2) + pltpu.roll(c, 1, 2))
+        return jnp.where(r_at < KZ, total - 6.0 * c, 0.0)
+
+    clane[...] = jnp.zeros(clane.shape, f32)
+    for a in range(3):
+        clane[:, :, 0:KZ] = cc_ref[a]
+        cbend[a] = BEND * laplace(laplace(clane[...]))
+
+    coarse_wait(2)
+    for kk in range(hz):
+        xrow[me[0], me[1], kk] = zrow[kk] + pltpu.roll(zrow[kk + hz], 64, 1)
+    coarse_start(1)
+
+    fine_wait(1)
     shape = (EX * PY, EX * PY)
     rows, cols = iota(shape, 0), iota(shape, 1)
     p_same = rows // PY == cols // PY
@@ -371,23 +453,59 @@
     low = jnp.where(p_same & (q == r + 2) & (r < 2), 1.0, 0.0)
     high = jnp.where(p_same & (q == r - (PY - 2)) & (r >= PY - 2), 1.0, 0.0)
     b_v[...] = a_v[0] + nn(agot[0], low) + nn(agot[1], high)
-
-    cslots[0, me[0]] = whole
-    whole = exchange(0, lambda side: b_v, bgot)
+    fine_start(0)
+
+    coarse_wait(1)
+    coarse_start(0)
+
+    fine_wait(0)
     shape = (PX * PY, EX * PY)
     rows, cols = iota(shape, 0), iota(shape, 1)
     own = jnp.where(cols == rows + 2 * PY, 1.0, 0.0)
     low = jnp.where((cols == rows + (PX + 2) * PY) & (rows < 2 * PY), 1.0, 0.0)
     high = jnp.where((cols == rows - (PX - 2) * PY) & (rows >= (PX - 2) * PY), 1.0, 0.0)
-    shape = (3 * KX * QC, 3 * KX * QC)
-    turned = nt(same(iota(shape, 0), iota(shape, 1)), whole)
     for a in range(3):
         part = slice(a * PZ, (a + 1) * PZ)
         out = nt(own, b_v[part]) + nt(low, bgot[0, part]) + nt(high, bgot[1, part])
         fo_ref[a] = out.reshape(PX, PY, PZ)
-        out = turned[a * KX * QC:(a + 1) * KX * QC] + bendc[a]
-        for p in range(KX):
-            co_ref[a, p] = out[p * QC:p * QC + KY, :]
+
+    coarse_wait(0)
+    sub, at = iota((ny, 128), 0), iota((ny, 128), 1)
+    for i in range(nx):
+        pages = []
+        for kk in range(hz):
+            page = jnp.broadcast_to(xrow[i, 0, kk], (ny, 128))
+            for j in range(1, ny):
+                page = jnp.where(sub == j, jnp.broadcast_to(xrow[i, j, kk], (ny, 128)), page)
+            pages.append(page)
+        for a in range(3):
+            for g in range(4):
+                c = 4 * a + g
+                value = None
+                for kk in range(hz):
+                    shift = (128 + 4 * kk - 4 * c) % 128
+                    moved = pages[kk] if shift == 0 else pltpu.roll(pages[kk], shift, 1)
+                    value = moved if kk == 0 else jnp.where(
+                        (at % 64) // 4 == kk, moved, value)
+                value = jnp.where(at < 4 * hz, value, pltpu.roll(value, 64 + 4 * hz, 1))
+                p = 2 * i + g // 2
+                part = pl.ds(g % 2, ny, stride=2)
+                co_ref[a, p, part, :] = (value + cbend[a, p, part, :])[:, 0:KZ]
+
+    for n in range(27):
+        if n != 13:
+            @pl.when(toward(sides[n])[0])
+            def _(n=n):
+                share_copy(n).wait_send()
+    for k in range(3):
+        for side in range(2):
+            @pl.when(has[k][side])
+            def _(k=k, side=side):
+                for piece in range(pieces if k == 1 else 1):
+                    halo(k, side, piece).wait_send()
+                fine_copy(k, side).wait_send()
+        for d in range(1, counts[k]):
+            coarse_copy(k, d).wait_send()
 
 
 def solution(mesh):
@@ -397,8 +515,8 @@
         SX, SY, SZ = warped.shape
         PX, PY, PZ = SX // SPF, SY // SPF, SZ // SPF
         KX, KY, KZ = coarse.shape[1:]
-        QC = KY
         EX, QE, RZ = PX + 4, 2 * PY, PZ + 8
+        CR = 48
         KC = SPF * SY
         most = max(sizes)
         vmem = pl.BlockSpec(memory_space=pltpu.VMEM)
@@ -417,17 +535,19 @@
                 V((SX + 4, SY + 16, SZ), f32),
                 V((2, SX, 2, SZ), f32), V((2, SX, 2, SZ), f32),
                 V((2, SY, SZ), f32), V((2, SY, SZ), f32), V((2, SY, SZ), f32),
-                V((2, 5 * QE, KC), bf16), V((SPC // SPF, 2, 4 * QC, KC), bf16),
+                V((2, 5 * QE, KC), bf16), V((SX // SPF, 2, CR, KC), bf16),
                 V((2, KC, 3 * SZ), bf16), V((2, KC, 3 * SZ), bf16),
-                V((2, EX, PY, 3 * SZ), f32), V((KX + 4, QC, 3 * SZ), f32),
+                V((2, EX, PY, 3 * SZ), f32), V((CR, 3 * SZ), f32),
                 V((2, 3, RZ, EX * PY), f32), V((2, 3, RZ, EX * PY), f32),
-                V((3, KX * QC, KZ), f32), V((3, KX * QC, KZ), f32),
+                V((KX, KY, 128), f32), V((3, KX, KY, 128), f32),
                 V((2, 2, 8, EX * PY), f32), V((2, 2, 8, EX * PY), f32),
                 V((2, 3 * PZ, EX * PY), f32), V((2, 3 * PZ, EX * PY), f32),
                 V((3 * PZ, EX * PY), f32), V((2, 3 * PZ, EX * PY), f32),
-                V((3, most, KZ, 3 * KX * QC), f32),
+                V((27, 1, 128), f32), V((27, 1, 128), f32),
+                V((sizes[2], 1, 128), f32),
+                V((sizes[0], sizes[1], sizes[2] // 2, 1, 128), f32),
                 D((2, SX // SPF)), D((2,)), D((3, 2)), D((3, 2)), D((2, 4)), D((2, 4)),
-                D((3, 2)), D((3, 2)), D((3, most)), D((3, most)),
+                D((3, 2)), D((3, 2)), D((27,)), D((27,)), D((3, most)), D((3, most)),
             ],
             compiler_params=pltpu.CompilerParams(
                 collective_id=0, has_side_effects=True, vmem_limit_bytes=66000000

time: 87.9 us -> 59.4 us (0.68)
  Pallas kernels: 83.1 us -> 55.3 us
    pallas_call x1, Pallas kernels: 83.1 us -> 55.3 us  [step(): pl.pallas_call(functools.partial(kernel, sizes), out_shape=(jax.ShapeDtyp...]
where the time goes in v1:
time: 59.4 us; the launch traced here: 59.2 us
  Pallas kernels  55.3 us (93%)
  local copies, waits for them, and re-layouts  3.31 us (6%)
  between operations  0.64 us (1%)
    pallas_call x1, Pallas kernels, step(): pl.pallas_call(functools.partial(kernel, sizes), out_shape=(jax.ShapeDtyp...  55.3 us
    unnamed x2, local copies, waits for them, and re-layouts  3.31 us

profile of v1, /device:TPU:1, one launch (start us, length us, event | category | flops | bytes accessed | tf_op | source)
XLA Modules:
  0.0 59.2 jit_solution(5275815838269037188)
XLA Ops:
  0.6 55.3 %shard_map.59 = (f32[3,8,8,16]{3,2,1,0:T(8,128)}, f32[3,16,16,32]{3,2,1,0:T(8,128)}) custom-call(f32[64,64,128]{2,1,0:T(8,128)} %w_hbm.1, f32[64,64,128]{2,1,0:T(8,128)} %f_hbm.1, f32[3,8,8,16]{3,2,1,0:T(8,128)} %fc_hbm.1, f32[3,16,16,32]{3,2,1,0:T(8,128)} %cc_hbm.1), custom_call_target="tpu_custom_call" | custom-call | tf_op jit(solution)/shard_map/pallas_call | solution.py:526
  55.9 1.5 %copy.8 = f32[3,8,8,16]{3,2,1,0:T(8,128)} copy(f32[3,8,8,16]{3,2,1,0:T(8,128)} %get-tuple-element.4) | data formatting | bytes 24576
  57.5 1.8 %copy.9 = f32[3,16,16,32]{3,2,1,0:T(8,128)} copy(f32[3,16,16,32]{3,2,1,0:T(8,128)} %get-tuple-element.5) | data formatting | bytes 196608

commit v2 on v1

--- a/solution.py
+++ b/solution.py
@@ -203,8 +203,9 @@
         ysend[0, x] = s[0:2]
         ysend[1, x] = s[SY - 2:SY]
         here = lane // 2 == x
-        low = jnp.where(here, pltpu.roll(s, 2 * x, 1), low)
-        high = jnp.where(here, pltpu.roll(s, lax.rem(2 * x + 2, SZ), 1), high)
+        low = jnp.where(here, pltpu.roll(s, 2 * x, 1) if x else s, low)
+        shift = (2 * x + 2) % SZ
+        high = jnp.where(here, pltpu.roll(s, shift, 1) if shift else s, high)
         return low, high
 
     carry = (jnp.zeros((SY, SZ), f32), jnp.zeros((SY, SZ), f32))
@@ -213,7 +214,8 @@
     for c in order:
         for copy in loads[c]:
             copy.wait()
-        carry = lax.fori_loop(c * SPF, (c + 1) * SPF, one_slab, carry)
+        for x in range(c * SPF, (c + 1) * SPF):
+            carry = one_slab(x, carry)
         done.add(c)
         for piece in range(pieces):
             inside = range(piece * each // SPF, (piece + 1) * each // SPF)
@@ -232,6 +234,30 @@
 
     accf[...] = jnp.zeros(accf.shape, f32)
     accc[...] = jnp.zeros(accc.shape, f32)
+
+    for copy in small:
+        copy.wait()
+    shape = (EX * QE, PX * PY)
+    rows, cols = iota(shape, 0), iota(shape, 1)
+    ox, oy = me[0] * PX, me[1] * PY
+    outer, inner = rows // (EX * PY), rows % (EX * PY)
+    planes = bend_planes(inner // PY - 2 + ox, ext_q(inner % PY + PY * outer) + oy,
+                         cols // PY + ox, cols % PY + oy, PX * nx, PY * ny)
+    RZ = tz_v.shape[2]
+
+    def ext_point(row):
+        return jnp.where(row < PZ, row, jnp.where(row < PZ + 2, row - PZ - 2, row - 2))
+
+    oz = me[2] * PZ
+    zr, zc = ext_point(iota((RZ, PZ), 0)) + oz, iota((RZ, PZ), 1) + oz
+    along = (same(zr, zc), diff1(zr, zc), diff2(zr, zc, PZ * nz))
+    for a in range(3):
+        block = fc_ref[a].reshape(PX * PY, PZ)
+        factors = [nn(plane, block) for plane in planes]
+        for half in range(2):
+            part = slice(half * EX * PY, (half + 1) * EX * PY)
+            bend_v[half, a] = (nt(along[0], factors[0][part]) + nt(along[1], factors[1][part])
+                               + nt(along[2], factors[2][part]))
 
     for k in (0, 1, 2):
         for side in range(2):
@@ -324,30 +350,6 @@
         def _(n=n):
             share_copy(n).start()
 
-    for copy in small:
-        copy.wait()
-    shape = (EX * QE, PX * PY)
-    rows, cols = iota(shape, 0), iota(shape, 1)
-    ox, oy = me[0] * PX, me[1] * PY
-    outer, inner = rows // (EX * PY), rows % (EX * PY)
-    planes = bend_planes(inner // PY - 2 + ox, ext_q(inner % PY + PY * outer) + oy,
-                         cols // PY + ox, cols % PY + oy, PX * nx, PY * ny)
-    RZ = tz_v.shape[2]
-
-    def ext_point(row):
-        return jnp.where(row < PZ, row, jnp.where(row < PZ + 2, row - PZ - 2, row - 2))
-
-    oz = me[2] * PZ
-    zr, zc = ext_point(iota((RZ, PZ), 0)) + oz, iota((RZ, PZ), 1) + oz
-    along = (same(zr, zc), diff1(zr, zc), diff2(zr, zc, PZ * nz))
-    for a in range(3):
-        block = fc_ref[a].reshape(PX * PY, PZ)
-        factors = [nn(plane, block) for plane in planes]
-        for half in range(2):
-            part = slice(half * EX * PY, (half + 1) * EX * PY)
-            bend_v[half, a] = (nt(along[0], factors[0][part]) + nt(along[1], factors[1][part])
-                               + nt(along[2], factors[2][part]))
-
     rows, cols = iota((RZ, SZ), 0), iota((RZ, SZ), 1)
     bz = weight(cols, ext_point(rows), SPF) * (SPF ** -1.5 / 24.0)
     for a in range(3):
@@ -375,21 +377,25 @@
             def _(side=side):
                 fine_copy(k, side).wait_recv()
 
-    hz = nz // 2
-    slots = (xrow.at[me[0]], xrow.at[me[0], me[1]], zrow.at[me[2]])
+    def coarse_slot(k, n):
+        if k == 0:
+            return xrow.at[n]
+        if k == 1:
+            return xrow.at[me[0], :, pl.ds(n, 1), :]
+        return zrow.at[:, pl.ds(n, 1), :]
 
     def coarse_copy(k, d):
         return pltpu.make_async_remote_copy(
-            src_ref=slots[k], dst_ref=slots[k],
+            src_ref=coarse_slot(k, me[k]), dst_ref=coarse_slot(k, me[k]),
             send_sem=cs_sem.at[k, d], recv_sem=cr_sem.at[k, d],
             device_id={axes[k]: lax.rem(me[k] + d, counts[k])}, device_id_type=MESH,
         )
 
     def coarse_from(k, d):
         other = lax.rem(me[k] + counts[k] - d, counts[k])
-        slot = (xrow.at[other], xrow.at[me[0], other], zrow.at[other])[k]
         return pltpu.make_async_remote_copy(
-            src_ref=slot, dst_ref=slot, send_sem=cs_sem.at[k, d], recv_sem=cr_sem.at[k, d],
+            src_ref=coarse_slot(k, other), dst_ref=coarse_slot(k, other),
+            send_sem=cs_sem.at[k, d], recv_sem=cr_sem.at[k, d],
             device_id={axes[k]: other}, device_id_type=MESH,
         )
 
@@ -413,7 +419,13 @@
     for n in range(27):
         if n != 13:
             own = own + crecv[n]
-    zrow[me[2]] = own
+    at = iota((1, 128), 1)
+    own = pltpu.roll(own, 4 * me[2], 1)
+    for a in range(3):
+        value = own if a == 0 else pltpu.roll(own, 128 - 16 * a, 1)
+        for g in range(1, 4):
+            value = jnp.where(at // 32 == g, pltpu.roll(own, (128 + 28 * g - 16 * a) % 128, 1), value)
+        zrow[a, pl.ds(me[2], 1), :] = jnp.where((at % 32) // 4 == me[2], value, 0.0)
     coarse_start(2)
 
     fine_wait(2)
@@ -441,8 +453,8 @@
         cbend[a] = BEND * laplace(laplace(clane[...]))
 
     coarse_wait(2)
-    for kk in range(hz):
-        xrow[me[0], me[1], kk] = zrow[kk] + pltpu.roll(zrow[kk + hz], 64, 1)
+    for a in range(3):
+        xrow[me[0], a, pl.ds(me[1], 1), :] = jnp.sum(zrow[a], axis=0, keepdims=True)
     coarse_start(1)
 
     fine_wait(1)
@@ -470,24 +482,11 @@
         fo_ref[a] = out.reshape(PX, PY, PZ)
 
     coarse_wait(0)
-    sub, at = iota((ny, 128), 0), iota((ny, 128), 1)
     for i in range(nx):
-        pages = []
-        for kk in range(hz):
-            page = jnp.broadcast_to(xrow[i, 0, kk], (ny, 128))
-            for j in range(1, ny):
-                page = jnp.where(sub == j, jnp.broadcast_to(xrow[i, j, kk], (ny, 128)), page)
-            pages.append(page)
         for a in range(3):
+            block = xrow[i, a]
             for g in range(4):
-                c = 4 * a + g
-                value = None
-                for kk in range(hz):
-                    shift = (128 + 4 * kk - 4 * c) % 128
-                    moved = pages[kk] if shift == 0 else pltpu.roll(pages[kk], shift, 1)
-                    value = moved if kk == 0 else jnp.where(
-                        (at % 64) // 4 == kk, moved, value)
-                value = jnp.where(at < 4 * hz, value, pltpu.roll(value, 64 + 4 * hz, 1))
+                value = block if g == 0 else pltpu.roll(block, 128 - 32 * g, 1)
                 p = 2 * i + g // 2
                 part = pl.ds(g % 2, ny, stride=2)
                 co_ref[a, p, part, :] = (value + cbend[a, p, part, :])[:, 0:KZ]
@@ -525,8 +524,7 @@
         D = pltpu.SemaphoreType.DMA
         return pl.pallas_call(
             functools.partial(kernel, sizes),
-            out_shape=(jax.ShapeDtypeStruct(fine.shape, f32),
-                       jax.ShapeDtypeStruct(coarse.shape, f32)),
+            out_shape=(V(fine.shape, f32), V(coarse.shape, f32)),
             in_specs=[hbm] * 4,
             out_specs=(vmem, vmem),
             scratch_shapes=[
@@ -544,8 +542,7 @@
                 V((2, 3 * PZ, EX * PY), f32), V((2, 3 * PZ, EX * PY), f32),
                 V((3 * PZ, EX * PY), f32), V((2, 3 * PZ, EX * PY), f32),
                 V((27, 1, 128), f32), V((27, 1, 128), f32),
-                V((sizes[2], 1, 128), f32),
-                V((sizes[0], sizes[1], sizes[2] // 2, 1, 128), f32),
+                V((3, sizes[2], 128), f32), V((sizes[0], 3, sizes[1], 128), f32),
                 D((2, SX // SPF)), D((2,)), D((3, 2)), D((3, 2)), D((2, 4)), D((2, 4)),
                 D((3, 2)), D((3, 2)), D((27,)), D((27,)), D((3, most)), D((3, most)),
             ],

time: 59.4 us -> 47.8 us (0.80)
  Pallas kernels: 55.3 us -> 45.7 us
  local copies, waits for them, and re-layouts: 3.31 us -> 1.39 us
    pallas_call x1, Pallas kernels: 55.3 us -> 45.7 us  [step(): pl.pallas_call(functools.partial(kernel, sizes), out_shape=(V(fine.shape,...]
    unnamed x2, local copies, waits for them, and re-layouts: 3.31 us -> 1.39 us
where the time goes in v2:
time: 47.8 us; the launch traced here: 47.7 us
  Pallas kernels  45.7 us (96%)
  local copies, waits for them, and re-layouts  1.39 us (3%)
  between operations  0.64 us (1%)
    pallas_call x1, Pallas kernels, step(): pl.pallas_call(functools.partial(kernel, sizes), out_shape=(V(fine.shape,...  45.7 us
    unnamed x2, local copies, waits for them, and re-layouts  1.39 us

profile of v2, /device:TPU:1, one launch (start us, length us, event | category | flops | bytes accessed | tf_op | source)
XLA Modules:
  0.0 47.7 jit_solution(4641137205986771608)
XLA Ops:
  0.6 45.7 %shard_map.59 = (f32[3,8,8,16]{3,2,1,0:T(8,128)S(1)}, f32[3,16,16,32]{3,2,1,0:T(8,128)S(1)}) custom-call(f32[64,64,128]{2,1,0:T(8,128)} %w_hbm.1, f32[64,64,128]{2,1,0:T(8,128)} %f_hbm.1, f32[3,8,8,16]{3,2,1,0:T(8,128)} %fc_hbm.1, f32[3,16,16,32]{3,2,1,0:T(8,128)} %cc_hbm.1), custom_call_target="tpu_custom_call" | custom-call | tf_op jit(solution)/shard_map/pallas_call | solution.py:525
  46.3 0.6 %copy.8 = f32[3,8,8,16]{3,2,1,0:T(8,128)} copy(f32[3,8,8,16]{3,2,1,0:T(8,128)S(1)} %get-tuple-element.2) | data formatting | bytes 24576
  46.9 0.7 %copy.9 = f32[3,16,16,32]{3,2,1,0:T(8,128)} copy(f32[3,16,16,32]{3,2,1,0:T(8,128)S(1)} %get-tuple-element.3) | data formatting | bytes 196608

commit v3 on v2

v3 whole, which is shorter than its diff:
```python
import functools

import jax
import jax.numpy as jnp
from jax import lax
from jax.experimental import pallas as pl
from jax.experimental.pallas import tpu as pltpu
from jax.sharding import PartitionSpec as P

SPF = 8
SPC = 32
BEND = 0.01
HI = lax.Precision.HIGHEST
MESH = pl.DeviceIdType.MESH
f32 = jnp.float32
bf16 = jnp.bfloat16


def nn(a, b):
    return lax.dot_general(
        a, b, (((1,), (0,)), ((), ())), precision=HI, preferred_element_type=f32
    )


def nt(a, b):
    return lax.dot_general(
        a, b, (((1,), (1,)), ((), ())), precision=HI, preferred_element_type=f32
    )


def spline(t):
    m = jnp.abs(t)
    inner = 2.0 / 3.0 - m * m + 0.5 * m * m * m
    r = 2.0 - m
    outer = r * r * r * (1.0 / 6.0)
    return jnp.where(m < 1.0, inner, jnp.where(m < 2.0, outer, 0.0))


def weight(voxel, point, spacing):
    scaled = (2 * voxel + 1 - spacing * (2 * point + 1)).astype(f32)
    return spline(scaled * (0.5 / spacing))


def iota(shape, axis):
    return lax.broadcasted_iota(jnp.int32, shape, axis)


def diff1(out, inp):
    d = jnp.abs(out - inp)
    return jnp.where(d == 0, -2.0, jnp.where(d == 1, 1.0, 0.0)).astype(f32)


def diff2(out, inp, count):
    d = jnp.abs(out - inp)
    edge = (inp == 0) | (inp == count - 1)
    centre = jnp.where(edge, 5.0, 6.0)
    return jnp.where(
        d == 0, centre, jnp.where(d == 1, -4.0, jnp.where(d == 2, 1.0, 0.0))
    ).astype(f32)


def same(out, inp):
    return jnp.where(out == inp, 1.0, 0.0).astype(f32)


def bend_planes(px, py, qx, qy, cx, cy):
    jx, jy = same(px, qx), same(py, qy)
    tx, ty = diff1(px, qx), diff1(py, qy)
    m0 = diff2(px, qx, cx) * jy + jx * diff2(py, qy, cy) + 2.0 * tx * ty
    m1 = 2.0 * (tx * jy + jx * ty)
    return m0 * BEND, m1 * BEND, jx * jy * BEND


def kernel(sizes, w_hbm, f_hbm, fc_hbm, cc_hbm, fo_ref, co_ref,
           w_v, f_v, fc_ref, cc_ref, s_v, xrecv, ysend, yrecv, yd, zsend, zrecv, zd,
           wf_v, wc_v, wy_v, wxe_v, fh_v, fl_v,
           accf, accc, tz_v, clane, cbend, zmsg, zgot, a_v, agot, b_v, bgot,
           cmsg, crecv, zrow, xrow, load_sem, small_sem, hs_sem, hr_sem,
           ms_sem, mr_sem, n_sem, cs_sem, cr_sem):
    nx, ny, nz = sizes
    axes = ("gx", "gy", "gz")
    counts = sizes
    me = [lax.axis_index(a) for a in axes]
    SX, SY, SZ = w_v.shape
    PX, PY, PZ = SX // SPF, SY // SPF, SZ // SPF
    KX, KY, KZ = cc_ref.shape[1:]
    EX, QE = PX + 4, 2 * PY
    CR = accc.shape[0]
    CQ, CX = 8, CR // 8
    RZ = tz_v.shape[2]
    KC = SPF * SY
    cells = SX // SPF
    lanes = 3 * SZ

    for c in range(cells):
        part = pl.ds(c * SPF, SPF)
        pltpu.make_async_copy(w_hbm.at[part], w_v.at[part], load_sem.at[c]).start()
        pltpu.make_async_copy(f_hbm.at[part], f_v.at[part], load_sem.at[c]).start()
    small = (pltpu.make_async_copy(fc_hbm, fc_ref, small_sem.at[0]),
             pltpu.make_async_copy(cc_hbm, cc_ref, small_sem.at[1]))
    for copy in small:
        copy.start()

    def load_wait(c):
        both = pl.ds(0, 2 * SPF)
        pltpu.make_async_copy(w_hbm.at[both], w_v.at[both], load_sem.at[c]).wait()

    has = [(me[k] > 0, me[k] < counts[k] - 1) for k in range(3)]
    sides = [(d, e, f) for f in range(3) for d in range(3) for e in range(3)]

    def toward(step):
        return {axes[k]: lax.rem(me[k] + (counts[k] + step[k] - 1), counts[k])
                for k in range(3) if step[k] != 1}

    def inside(step):
        ok = None
        for k in range(3):
            if step[k] != 1:
                here = has[k][0] if step[k] == 0 else has[k][1]
                ok = here if ok is None else ok & here
        return ok

    def far_first(n):
        return sorted(range(1, n), key=lambda d: -min(d, n - d))

    barrier = pltpu.get_barrier_semaphore()
    total = 0
    for k, a in enumerate(axes):
        for d in far_first(counts[k]):
            pl.semaphore_signal(
                barrier, inc=1, device_id={a: lax.rem(me[k] + d, counts[k])}, device_id_type=MESH
            )
            total += 1
    for step in sides:
        if sum(n != 1 for n in step) >= 2:
            pl.semaphore_signal(barrier, inc=1, device_id=toward(step), device_id_type=MESH)
            total += 1

    zero_plane = jnp.zeros((2, SY, SZ), f32)
    s_v[0:2, 8:8 + SY, :] = zero_plane
    s_v[SX + 2:SX + 4, 8:8 + SY, :] = zero_plane
    zero_rows = jnp.zeros((SX, 2, SZ), f32)
    s_v[2:SX + 2, 6:8, :] = zero_rows
    s_v[2:SX + 2, 8 + SY:10 + SY, :] = zero_rows

    def split_store(ref, index, value):
        high = value.astype(bf16)
        ref[index + (0,)] = high
        ref[index + (1,)] = (value - high.astype(f32)).astype(bf16)

    def ext_q(q):
        return jnp.where(q < PY, q, jnp.where(q < PY + 2, q - PY - 2, q - 2))

    def outer(along_x, along_y):
        return jnp.concatenate([along_x[p:p + 1] * along_y for p in range(along_x.shape[0])], axis=0)

    col = iota((8, KC), 1)
    col2 = iota((QE, KC), 1)
    split_store(wf_v, (), outer(weight(col // SY, iota((8, KC), 0) - 2, SPF)[0:5],
                                weight(col2 % SY, ext_q(iota((QE, KC), 0)), SPF)))
    along_y = weight(col % SY, iota((8, KC), 0) - 2, SPC)
    for c in range(cells):
        split_store(wc_v, (c,), outer(
            weight(col // SY + c * SPF, iota((8, KC), 0) - 2, SPC)[0:CX], along_y))
    col, row = iota((QE, 4 * SX), 1), iota((QE, 4 * SX), 0)
    face_x, face_y = (col % (2 * SX)) // 2, col % 2 + (SY - 2) * (col // (2 * SX))
    along_x = weight(face_x, row - 2, SPF)[0:EX]
    along_y = weight(face_y, ext_q(row), SPF)
    split_store(wy_v, (), jnp.concatenate([
        outer(along_x, along_y[0:PY]), outer(along_x, along_y[PY:QE]),
        outer(weight(face_x, row - 2, SPC)[0:CX], weight(face_y, row - 2, SPC)[0:CQ])], axis=0))
    row, col = iota((4 * SX, 128), 0), iota((4 * SX, 128), 1)
    face_x = (row % (2 * SX)) // 2
    place = row % 2 + 2 - 2 * (row // (2 * SX))
    wxe_v[...] = jnp.where(col % 4 == place, jnp.where(
        col < 64, weight(face_x, col // 4 - 2, SPF), weight(face_x, col // 4 - 18, SPC)), 0.0)
    accf[...] = jnp.zeros(accf.shape, f32)
    accc[...] = jnp.zeros(accc.shape, f32)

    lane = iota((SY, SZ), 1)
    packs = [jnp.zeros((SY, SZ), f32) for _ in range(4)]
    for c in range(cells):
        load_wait(c)
        for x in range(c * SPF, (c + 1) * SPF):
            w, f = w_v[x], f_v[x]
            s, d = w + f, w - f
            s_v[x + 2, 8:8 + SY, :] = s
            for side, part in ((0, slice(0, 2)), (1, slice(SY - 2, SY))):
                ysend[side, 2 * x:2 * x + 2, :] = s[part]
                yd[side, 2 * x:2 * x + 2, :] = d[part]
            here = lane // 2 == x
            for n, value in enumerate((s, s, d, d)):
                shift = (2 * x + 2 * (n % 2)) % SZ
                moved = pltpu.roll(value, shift, 1) if shift else value
                packs[n] = jnp.where(here, moved, packs[n])
    for side in range(2):
        zsend[side] = packs[side]
        zd[side] = packs[2 + side]

    pl.semaphore_wait(barrier, total)

    def neighbour_copy(k, side, src, dst, send, recv):
        step = [1, 1, 1]
        step[k] = 2 * side
        return pltpu.make_async_remote_copy(
            src_ref=src, dst_ref=dst, send_sem=send, recv_sem=recv,
            device_id=toward(step), device_id_type=MESH,
        )

    def halo(k, side):
        if k == 0:
            src = s_v.at[pl.ds(2 if side == 0 else SX, 2), pl.ds(8, SY), :]
        else:
            src = (ysend if k == 1 else zsend).at[side]
        return neighbour_copy(k, side, src, (xrecv, yrecv, zrecv)[k].at[1 - side],
                              hs_sem.at[k], hr_sem.at[k])

    def whole(k, ref, send, recv):
        return neighbour_copy(k, 0, ref, ref, send, recv)

    for k in (1, 2, 0):
        for side in range(2):
            halo(k, side).start()

    def forces(i):
        slot = i % 2
        T = 16
        for xx in range(SPF):
            x = i * SPF + xx
            for r in range(0, SY, T):
                at = 8 + r
                d = w_v[x, r:r + T, :] - f_v[x, r:r + T, :]
                s = s_v[x + 2, at:at + T, :]
                gx = (s_v[x, at:at + T, :] - s_v[x + 4, at:at + T, :]
                      + 8.0 * (s_v[x + 3, at:at + T, :] - s_v[x + 1, at:at + T, :]))
                gy = (s_v[x + 2, at - 2:at - 2 + T, :] - s_v[x + 2, at + 2:at + 2 + T, :]
                      + 8.0 * (s_v[x + 2, at + 1:at + 1 + T, :] - s_v[x + 2, at - 1:at - 1 + T, :]))
                gz = (pltpu.roll(s, 2, 1) - pltpu.roll(s, SZ - 2, 1)
                      + 8.0 * (pltpu.roll(s, SZ - 1, 1) - pltpu.roll(s, 1, 1)))
                row = xx * SY + r
                for a, g in enumerate((gx, gy, gz)):
                    force = g * d
                    high = force.astype(bf16)
                    fh_v[slot, row:row + T, a * SZ:(a + 1) * SZ] = high
                    fl_v[slot, row:row + T, a * SZ:(a + 1) * SZ] = (
                        force - high.astype(f32)).astype(bf16)

    def cell_weights(i):
        return jnp.concatenate([wf_v[0], wc_v[i, 0], wf_v[1], wc_v[i, 1]], axis=0)

    def project(weights, high, low):
        many = weights.shape[0] // 2
        both = jnp.dot(weights, high, preferred_element_type=f32)
        return both[:many] + both[many:] + jnp.dot(
            weights[:many], low, preferred_element_type=f32)

    def collect(i, out, part):
        fine = out[:5 * QE].reshape(5, 2, PY, out.shape[1])
        accf[0, i:i + 5, :, part] += fine[:, 0]
        accf[1, i:i + 5, :, part] += fine[:, 1]
        accc[:, part] += out[5 * QE:]

    def gather(i):
        slot = i % 2
        collect(i, project(cell_weights(i), fh_v[slot], fl_v[slot]), slice(0, lanes))

    forces(0)
    for i in range(cells):
        if i + 1 < cells:
            forces(i + 1)
        gather(i)

    for k, got in enumerate((xrecv, yrecv, zrecv)):
        whole(k, got, hs_sem.at[k], hr_sem.at[k]).wait_recv()

    gate = [[jnp.where(h, 1.0, 0.0) for h in pair] for pair in has]

    def split(value):
        high = value.astype(bf16)
        return high, (value - high.astype(f32)).astype(bf16)

    def diff(x):
        return w_v[x] - f_v[x]

    for side, i in ((0, 0), (1, cells - 1)):
        r0, r1 = xrecv[side, 0] * gate[0][side], xrecv[side, 1] * gate[0][side]
        if side == 0:
            face = jnp.concatenate([(r0 - 8.0 * r1) * diff(0), r1 * diff(1)], axis=0)
            part = slice(0, 2 * SY)
        else:
            face = jnp.concatenate([-r0 * diff(SX - 2), (8.0 * r0 - r1) * diff(SX - 1)], axis=0)
            part = slice(KC - 2 * SY, KC)
        collect(i, project(cell_weights(i)[:, part], *split(face)), slice(0, SZ))

    rows = iota((SX // 4, 8, SZ), 1) % 2 == 0
    r = (yrecv[0] * gate[1][0]).reshape(SX // 4, 8, SZ)
    low = jnp.where(rows, r - 8.0 * pltpu.roll(r, 7, 1), r).reshape(2 * SX, SZ) * yd[0]
    r = (yrecv[1] * gate[1][1]).reshape(SX // 4, 8, SZ)
    high = jnp.where(rows, -r, 8.0 * pltpu.roll(r, 1, 1) - r).reshape(2 * SX, SZ) * yd[1]
    out = project(jnp.concatenate([wy_v[0], wy_v[1]], axis=0),
                  *split(jnp.concatenate([low, high], axis=0)))
    for half in range(2):
        accf[half, :, :, SZ:2 * SZ] += out[half * EX * PY:(half + 1) * EX * PY].reshape(EX, PY, SZ)
    accc[:, SZ:2 * SZ] += out[2 * EX * PY:]

    even = lane % 2 == 0
    dl = zrecv[0] * gate[2][0] - zsend[1]
    dh = zrecv[1] * gate[2][1] - zsend[0]
    low = jnp.where(even, dl - 8.0 * pltpu.roll(dl, SZ - 1, 1), dl) * zd[0]
    high = jnp.where(even, -dh, 8.0 * pltpu.roll(dh, 1, 1) - dh) * zd[1]
    row, col = iota((QE + CQ, SY), 0), iota((QE + CQ, SY), 1)
    along_y = jnp.where(row < QE, weight(col, ext_q(row), SPF), weight(col, row - QE - 2, SPC))
    out = nn(nn(along_y, jnp.concatenate([low, high], axis=1)), wxe_v[...])
    at = iota((PY, SZ), 1)
    edge = (at < 2) | (at >= SZ - 2)

    def spread(half, shift):
        return jnp.where(edge, pltpu.roll(out[half * PY:(half + 1) * PY], shift % 128, 1), 0.0)

    for p in range(EX):
        for half in range(2):
            accf[half, p, :, 2 * SZ:3 * SZ] += spread(half, 254 - 4 * p)
    for p in range(CX):
        accc[p * CQ:(p + 1) * CQ, 2 * SZ:3 * SZ] += spread(2, 254 - 64 - 4 * p)

    rows, cols = iota((SZ, 128), 0), iota((SZ, 128), 1)
    bzc = weight(rows, cols % 4 + 4 * (cols // 16 - 1), SPC) * (SPC ** -1.5 / 24.0)
    stack = jnp.concatenate([accc[:, a * SZ:(a + 1) * SZ] for a in range(3)], axis=0)
    shares = nn(stack, bzc)
    rows, cols = iota((CR, 128), 0), iota((CR, 128), 1)
    keep = ((cols // 4) % 4 == 2 * ((rows // CQ) % 2) + rows % 2) & (cols < 48)
    for f in range(3):
        value = shares[0:CR]
        value = value if f == 0 else pltpu.roll(value, 128 - 16 * f, 1)
        for a in (1, 2):
            moved = shares[a * CR:(a + 1) * CR]
            moved = moved if a == f else pltpu.roll(moved, (128 + 16 * (a - f)) % 128, 1)
            value = jnp.where(cols // 16 == a, moved, value)
        value = jnp.where(keep, value, 0.0).reshape(3, 2, CQ, 128)
        value = value[:, 0] + value[:, 1]
        value = value + pltpu.roll(value, 7, 1)
        for d in range(3):
            for e in range(3):
                cmsg[f * 9 + d * 3 + e] = value[d, 2 * e:2 * e + 1, :]

    others = [n for n in range(27) if n != 13]
    for n in sorted(others, key=lambda n: -sum(v != 1 for v in sides[n])):
        pltpu.make_async_remote_copy(
            src_ref=cmsg.at[n], dst_ref=crecv.at[others.index(26 - n)],
            send_sem=n_sem.at[0], recv_sem=n_sem.at[1],
            device_id=toward(sides[n]), device_id_type=MESH,
        ).start()

    rows, cols = iota((RZ, SZ), 0), iota((RZ, SZ), 1)

    def ext_point(row):
        return jnp.where(row < PZ, row, jnp.where(row < PZ + 2, row - PZ - 2, row - 2))

    bz = weight(cols, ext_point(rows), SPF) * (SPF ** -1.5 / 24.0)
    for a in range(3):
        for half in range(2):
            block = accf[half, :, :, a * SZ:(a + 1) * SZ].reshape(EX * PY, SZ)
            tz_v[half, a] = nt(bz, block)

    for copy in small:
        copy.wait()
    shape = (PX * PY, EX * QE)
    rows, cols = iota(shape, 0), iota(shape, 1)
    ox, oy, oz = me[0] * PX, me[1] * PY, me[2] * PZ
    wide, inner = cols // (EX * PY), cols % (EX * PY)
    planes = bend_planes(inner // PY - 2 + ox, ext_q(inner % PY + PY * wide) + oy,
                         rows // PY + ox, rows % PY + oy, PX * nx, PY * ny)
    zr, zc = ext_point(iota((RZ, PZ), 0)) + oz, iota((RZ, PZ), 1) + oz
    along = jnp.concatenate([same(zr, zc), diff1(zr, zc), diff2(zr, zc, PZ * nz)], axis=0)
    turned = nt(along, fc_ref[...].reshape(3 * PX * PY, PZ))
    turned = jnp.concatenate([jnp.concatenate([
        turned[k * RZ:(k + 1) * RZ, a * PX * PY:(a + 1) * PX * PY] for k in range(3)], axis=1)
        for a in range(3)], axis=0)
    bent = nn(turned, jnp.concatenate(planes, axis=0))
    for a in range(3):
        for half in range(2):
            tz_v[half, a] += bent[a * RZ:(a + 1) * RZ, half * EX * PY:(half + 1) * EX * PY]
            for side in range(2):
                zmsg[side, half, 2 * a:2 * a + 2, :] = tz_v[
                    half, a, PZ + 2 * side:PZ + 2 * side + 2, :]

    def fine_start(k):
        for side in range(2):
            source = (b_v, a_v.at[1], zmsg.at[side])[k]
            neighbour_copy(k, side, source, (bgot, agot, zgot)[k].at[1 - side],
                           ms_sem.at[k], mr_sem.at[k]).start()

    def fine_whole(k):
        return whole(k, (bgot, agot, zgot)[k], ms_sem.at[k], mr_sem.at[k])

    def coarse_slot(k, n):
        if k == 0:
            return xrow.at[n]
        if k == 1:
            return xrow.at[me[0], :, pl.ds(n, 1), :]
        return zrow.at[:, pl.ds(n, 1), :]

    def coarse_start(k):
        for d in far_first(counts[k]):
            pltpu.make_async_remote_copy(
                src_ref=coarse_slot(k, me[k]), dst_ref=coarse_slot(k, me[k]),
                send_sem=cs_sem.at[k], recv_sem=cr_sem.at[k],
                device_id={axes[k]: lax.rem(me[k] + d, counts[k])}, device_id_type=MESH,
            ).start()

    def coarse_whole(k):
        part = pl.ds(0, counts[k] - 1)
        ref = (xrow.at[part], xrow.at[me[0], :, part, :], zrow.at[:, part, :])[k]
        return whole(k, ref, cs_sem.at[k], cr_sem.at[k])

    fine_start(2)

    whole(0, crecv, n_sem.at[0], n_sem.at[1]).wait_recv()
    own = cmsg[13]
    for n in others:
        own = own + jnp.where(inside(sides[n]), crecv[others.index(n)], 0.0)
    at = iota((1, 128), 1)
    own = pltpu.roll(own, 4 * me[2], 1)
    for a in range(3):
        value = own if a == 0 else pltpu.roll(own, 128 - 16 * a, 1)
        for g in range(1, 4):
            value = jnp.where(at // 32 == g, pltpu.roll(own, (128 + 28 * g - 16 * a) % 128, 1), value)
        zrow[a, pl.ds(me[2], 1), :] = jnp.where((at % 32) // 4 == me[2], value, 0.0)
    coarse_start(2)

    q_at, r_at = iota((KX, KY, 128), 1), iota((KX, KY, 128), 2)

    def laplace(c):
        zero = jnp.zeros((1, KY, 128), f32)
        total = (jnp.concatenate([c[1:], zero], axis=0) + jnp.concatenate([zero, c[:-1]], axis=0)
                 + jnp.where(q_at < KY - 1, pltpu.roll(c, KY - 1, 1), 0.0)
                 + jnp.where(q_at > 0, pltpu.roll(c, 1, 1), 0.0)
                 + pltpu.roll(c, 127, 2) + pltpu.roll(c, 1, 2))
        return jnp.where(r_at < KZ, total - 6.0 * c, 0.0)

    clane[...] = jnp.zeros(clane.shape, f32)
    for a in range(3):
        clane[:, :, 0:KZ] = cc_ref[a]
        cbend[a] = BEND * laplace(laplace(clane[...]))

    coarse_whole(2).wait_recv()
    for a in range(3):
        xrow[me[0], a, pl.ds(me[1], 1), :] = jnp.sum(zrow[a], axis=0, keepdims=True)
    coarse_start(1)

    fine_whole(2).wait_recv()
    for half in range(2):
        for a in range(3):
            part = slice(2 * a, 2 * a + 2)
            tz_v[half, a, 0:2, :] = tz_v[half, a, 0:2, :] + zgot[0, half, part, :] * gate[2][0]
            tz_v[half, a, PZ - 2:PZ, :] = (
                tz_v[half, a, PZ - 2:PZ, :] + zgot[1, half, part, :] * gate[2][1])
            a_v[half, a * PZ:(a + 1) * PZ, :] = tz_v[half, a, 0:PZ, :]
    fine_start(1)

    coarse_whole(1).wait_recv()
    coarse_start(0)

    fine_whole(1).wait_recv()
    shape = (EX * PY, EX * PY)
    rows, cols = iota(shape, 0), iota(shape, 1)
    p_same = rows // PY == cols // PY
    q, r = rows % PY, cols % PY
    low = jnp.where(p_same & (q == r + 2) & (r < 2), 1.0, 0.0)
    high = jnp.where(p_same & (q == r - (PY - 2)) & (r >= PY - 2), 1.0, 0.0)
    b_v[...] = (a_v[0] + nn(agot[0] * gate[1][0], low) + nn(agot[1] * gate[1][1], high))
    fine_start(0)

    fine_whole(0).wait_recv()
    shape = (PX * PY, EX * PY)
    rows, cols = iota(shape, 0), iota(shape, 1)
    own = jnp.where(cols == rows + 2 * PY, 1.0, 0.0)
    low = jnp.where((cols == rows + (PX + 2) * PY) & (rows < 2 * PY), gate[0][0], 0.0)
    high = jnp.where((cols == rows - (PX - 2) * PY) & (rows >= (PX - 2) * PY), gate[0][1], 0.0)
    for a in range(3):
        part = slice(a * PZ, (a + 1) * PZ)
        out = nt(own, b_v[part]) + nt(low, bgot[0, part]) + nt(high, bgot[1, part])
        fo_ref[a] = out.reshape(PX, PY, PZ)

    for k, got in enumerate((xrecv, yrecv, zrecv)):
        whole(k, got, hs_sem.at[k], hr_sem.at[k]).wait_send()
        fine_whole(k).wait_send()
        coarse_whole(k).wait_send()
    whole(0, crecv, n_sem.at[0], n_sem.at[1]).wait_send()

    coarse_whole(0).wait_recv()
    for i in range(nx):
        for a in range(3):
            block = xrow[i, a]
            for g in range(4):
                value = block if g == 0 else pltpu.roll(block, 128 - 32 * g, 1)
                p = 2 * i + g // 2
                part = pl.ds(g % 2, ny, stride=2)
                co_ref[a, p, part, :] = (value + cbend[a, p, part, :])[:, 0:KZ]


def solution(mesh):
    sizes = tuple(mesh.shape[a] for a in ("gx", "gy", "gz"))

    def step(warped, fixed, fine, coarse):
        SX, SY, SZ = warped.shape
        PX, PY, PZ = SX // SPF, SY // SPF, SZ // SPF
        KX, KY, KZ = coarse.shape[1:]
        EX, QE, RZ = PX + 4, 2 * PY, PZ + 8
        CR = 48
        KC = SPF * SY
        vmem = pl.BlockSpec(memory_space=pltpu.VMEM)
        hbm = pl.BlockSpec(memory_space=pltpu.HBM)
        V = pltpu.VMEM
        D = pltpu.SemaphoreType.DMA
        return pl.pallas_call(
            functools.partial(kernel, sizes),
            out_shape=(V(fine.shape, f32), V(coarse.shape, f32)),
            in_specs=[hbm] * 4,
            out_specs=(vmem, vmem),
            scratch_shapes=[
                V((SX, SY, SZ), f32), V((SX, SY, SZ), f32),
                V((3, PX, PY, PZ), f32), V(coarse.shape, f32),
                V((SX + 4, SY + 16, SZ), f32), V((2, 2, SY, SZ), f32),
                V((2, 2 * SX, SZ), f32), V((2, 2 * SX, SZ), f32), V((2, 2 * SX, SZ), f32),
                V((2, SY, SZ), f32), V((2, SY, SZ), f32), V((2, SY, SZ), f32),
                V((2, 5 * QE, KC), bf16), V((SX // SPF, 2, CR, KC), bf16),
                V((2, EX * QE + CR, 4 * SX), bf16), V((4 * SX, 128), f32),
                V((2, KC, 3 * SZ), bf16), V((2, KC, 3 * SZ), bf16),
                V((2, EX, PY, 3 * SZ), f32), V((CR, 3 * SZ), f32),
                V((2, 3, RZ, EX * PY), f32),
                V((KX, KY, 128), f32), V((3, KX, KY, 128), f32),
                V((2, 2, 8, EX * PY), f32), V((2, 2, 8, EX * PY), f32),
                V((2, 3 * PZ, EX * PY), f32), V((2, 3 * PZ, EX * PY), f32),
                V((3 * PZ, EX * PY), f32), V((2, 3 * PZ, EX * PY), f32),
                V((27, 1, 128), f32), V((26, 1, 128), f32),
                V((3, sizes[2], 128), f32), V((sizes[0], 3, sizes[1], 128), f32),
                D((SX // SPF,)), D((2,)), D((3,)), D((3,)),
                D((3,)), D((3,)), D((2,)), D((3,)), D((3,)),
            ],
            compiler_params=pltpu.CompilerParams(
                collective_id=0, has_side_effects=True, vmem_limit_bytes=66000000
            ),
        )(warped, fixed, fine, coarse)

    in_specs = (P("gx", "gy", "gz"), P("gx", "gy", "gz"), P(None, "gx", "gy", "gz"), P())
    out_specs = (P(None, "gx", "gy", "gz"), P())
    return jax.shard_map(
        step, mesh=mesh, in_specs=in_specs, out_specs=out_specs, check_vma=False
    )
```

time: 47.8 us -> 40.8 us (0.85)
  Pallas kernels: 45.7 us -> 38.7 us
    pallas_call x1, Pallas kernels: 45.7 us -> 38.7 us  [step(): pl.pallas_call(functools.partial(kernel, sizes), out_shape=(V(fine.shape,...]
where the time goes in v3:
time: 40.8 us; the launch traced here: 40.7 us
  Pallas kernels  38.7 us (95%)
  local copies, waits for them, and re-layouts  1.39 us (3%)
  between operations  0.64 us (2%)
    pallas_call x1, Pallas kernels, step(): pl.pallas_call(functools.partial(kernel, sizes), out_shape=(V(fine.shape,...  38.7 us
    unnamed x2, local copies, waits for them, and re-layouts  1.39 us

profile of v3, /device:TPU:1, one launch (start us, length us, event | category | flops | bytes accessed | tf_op | source)
XLA Modules:
  0.0 40.7 jit_solution(6753904834729018596)
XLA Ops:
  0.6 38.7 %shard_map.59 = (f32[3,8,8,16]{3,2,1,0:T(8,128)S(1)}, f32[3,16,16,32]{3,2,1,0:T(8,128)S(1)}) custom-call(f32[64,64,128]{2,1,0:T(8,128)} %w_hbm.1, f32[64,64,128]{2,1,0:T(8,128)} %f_hbm.1, f32[3,8,8,16]{3,2,1,0:T(8,128)} %fc_hbm.1, f32[3,16,16,32]{3,2,1,0:T(8,128)} %cc_hbm.1), custom_call_target="tpu_custom_call" | custom-call | tf_op jit(solution)/shard_map/pallas_call | solution.py:516
  39.3 0.6 %copy.8 = f32[3,8,8,16]{3,2,1,0:T(8,128)} copy(f32[3,8,8,16]{3,2,1,0:T(8,128)S(1)} %get-tuple-element.2) | data formatting | bytes 24576
  39.9 0.7 %copy.9 = f32[3,16,16,32]{3,2,1,0:T(8,128)} copy(f32[3,16,16,32]{3,2,1,0:T(8,128)S(1)} %get-tuple-element.3) | data formatting | bytes 196608

commit v4 on v3

--- a/solution.py
+++ b/solution.py
@@ -73,7 +73,7 @@
 
 def kernel(sizes, w_hbm, f_hbm, fc_hbm, cc_hbm, fo_ref, co_ref,
            w_v, f_v, fc_ref, cc_ref, s_v, xrecv, ysend, yrecv, yd, zsend, zrecv, zd,
-           wf_v, wc_v, wy_v, wxe_v, fh_v, fl_v,
+           wf_v, wc_v, wy_v, wxe_v, bzc_v, pz_v, gz_v, zp_v,
            accf, accc, tz_v, clane, cbend, zmsg, zgot, a_v, agot, b_v, bgot,
            cmsg, crecv, zrow, xrow, load_sem, small_sem, hs_sem, hr_sem,
            ms_sem, mr_sem, n_sem, cs_sem, cr_sem):
@@ -170,32 +170,57 @@
         outer(along_x, along_y[0:PY]), outer(along_x, along_y[PY:QE]),
         outer(weight(face_x, row - 2, SPC)[0:CX], weight(face_y, row - 2, SPC)[0:CQ])], axis=0))
     row, col = iota((4 * SX, 128), 0), iota((4 * SX, 128), 1)
-    face_x = (row % (2 * SX)) // 2
+    face_x = (row % (2 * SX)) // 4 + jnp.where(row % 4 < 2, SX // 2, 0)
     place = row % 2 + 2 - 2 * (row // (2 * SX))
     wxe_v[...] = jnp.where(col % 4 == place, jnp.where(
         col < 64, weight(face_x, col // 4 - 2, SPF), weight(face_x, col // 4 - 18, SPC)), 0.0)
+    row, col = iota((2 * SZ, 2 * SZ), 0) % SZ, iota((2 * SZ, 2 * SZ), 1)
+    away = row - col
+    slope = jnp.where(away == 1, 8.0, jnp.where(away == -1, -8.0, jnp.where(
+        away == -2, 1.0, jnp.where(away == 2, -1.0, 0.0))))
+    pick = jnp.where(row == (col % 4 + SZ - 2) % SZ, 1.0, 0.0)
+    pz_v[...] = jnp.where(col < SZ, slope, pick).astype(bf16)
+    rows, cols = iota((SZ, 128), 0), iota((SZ, 128), 1)
+    bzc_v[...] = weight(rows, cols % 4 + 4 * (cols // 16 - 1), SPC) * (SPC ** -1.5 / 24.0)
     accf[...] = jnp.zeros(accf.shape, f32)
     accc[...] = jnp.zeros(accc.shape, f32)
 
     lane = iota((SY, SZ), 1)
-    packs = [jnp.zeros((SY, SZ), f32) for _ in range(4)]
+    half_x = SX // 2
+
+    def split(value):
+        high = value.astype(bf16)
+        return high, (value - high.astype(f32)).astype(bf16)
+
     for c in range(cells):
         load_wait(c)
+        wide = ([], [])
         for x in range(c * SPF, (c + 1) * SPF):
             w, f = w_v[x], f_v[x]
             s, d = w + f, w - f
             s_v[x + 2, 8:8 + SY, :] = s
+            w_v[x] = d
             for side, part in ((0, slice(0, 2)), (1, slice(SY - 2, SY))):
                 ysend[side, 2 * x:2 * x + 2, :] = s[part]
                 yd[side, 2 * x:2 * x + 2, :] = d[part]
-            here = lane // 2 == x
-            for n, value in enumerate((s, s, d, d)):
-                shift = (2 * x + 2 * (n % 2)) % SZ
-                moved = pltpu.roll(value, shift, 1) if shift else value
-                packs[n] = jnp.where(here, moved, packs[n])
-    for side in range(2):
-        zsend[side] = packs[side]
-        zd[side] = packs[2 + side]
+            for n, value in enumerate((s, d)):
+                wide[n].append(jnp.concatenate(split(value), axis=1))
+        out = jnp.dot(jnp.concatenate(wide[0], axis=0), pz_v[...], preferred_element_type=f32)
+        gz_v[c] = out[:, 0:SZ]
+        picked = (out[:, SZ:2 * SZ],
+                  jnp.dot(jnp.concatenate(wide[1], axis=0), pz_v[:, SZ:2 * SZ], preferred_element_type=f32))
+        tile = c * SPF // half_x
+        for n in range(2):
+            pack = None if c * SPF % half_x == 0 else zp_v[n, tile]
+            for xx in range(SPF):
+                value = picked[n][xx * SY:(xx + 1) * SY]
+                here = lane // 4 == (c * SPF + xx) % half_x
+                pack = value if pack is None else jnp.where(here, value, pack)
+            zp_v[n, tile] = pack
+    upper = lane % 4 >= 2
+    for n, ref in enumerate((zsend, zd)):
+        ref[0] = jnp.where(upper, zp_v[n, 0], pltpu.roll(zp_v[n, 1], SZ - 2, 1))
+        ref[1] = jnp.where(upper, pltpu.roll(zp_v[n, 0], 2, 1), zp_v[n, 1])
 
     pl.semaphore_wait(barrier, total)
 
@@ -223,27 +248,25 @@
             halo(k, side).start()
 
     def forces(i):
-        slot = i % 2
         T = 16
-        for xx in range(SPF):
-            x = i * SPF + xx
-            for r in range(0, SY, T):
-                at = 8 + r
-                d = w_v[x, r:r + T, :] - f_v[x, r:r + T, :]
-                s = s_v[x + 2, at:at + T, :]
-                gx = (s_v[x, at:at + T, :] - s_v[x + 4, at:at + T, :]
-                      + 8.0 * (s_v[x + 3, at:at + T, :] - s_v[x + 1, at:at + T, :]))
+        tiles = {}
+        for r in range(0, SY, T):
+            at = 8 + r
+            near = [s_v[i * SPF + n, at:at + T, :] for n in range(4)]
+            for xx in range(SPF):
+                x = i * SPF + xx
+                near.append(s_v[x + 4, at:at + T, :])
+                d = w_v[x, r:r + T, :]
+                gx = near[0] - near[4] + 8.0 * (near[3] - near[1])
+                near.pop(0)
                 gy = (s_v[x + 2, at - 2:at - 2 + T, :] - s_v[x + 2, at + 2:at + 2 + T, :]
                       + 8.0 * (s_v[x + 2, at + 1:at + 1 + T, :] - s_v[x + 2, at - 1:at - 1 + T, :]))
-                gz = (pltpu.roll(s, 2, 1) - pltpu.roll(s, SZ - 2, 1)
-                      + 8.0 * (pltpu.roll(s, SZ - 1, 1) - pltpu.roll(s, 1, 1)))
                 row = xx * SY + r
-                for a, g in enumerate((gx, gy, gz)):
-                    force = g * d
-                    high = force.astype(bf16)
-                    fh_v[slot, row:row + T, a * SZ:(a + 1) * SZ] = high
-                    fl_v[slot, row:row + T, a * SZ:(a + 1) * SZ] = (
-                        force - high.astype(f32)).astype(bf16)
+                gz = gz_v[i, row:row + T, :]
+                tiles[row] = [split(g * d) for g in (gx, gy, gz)]
+        return [jnp.concatenate([
+            jnp.concatenate([tiles[row][a][n] for row in sorted(tiles)], axis=0)
+            for a in range(3)], axis=1) for n in range(2)]
 
     def cell_weights(i):
         return jnp.concatenate([wf_v[0], wc_v[i, 0], wf_v[1], wc_v[i, 1]], axis=0)
@@ -260,27 +283,16 @@
         accf[1, i:i + 5, :, part] += fine[:, 1]
         accc[:, part] += out[5 * QE:]
 
-    def gather(i):
-        slot = i % 2
-        collect(i, project(cell_weights(i), fh_v[slot], fl_v[slot]), slice(0, lanes))
-
-    forces(0)
     for i in range(cells):
-        if i + 1 < cells:
-            forces(i + 1)
-        gather(i)
+        collect(i, project(cell_weights(i), *forces(i)), slice(0, lanes))
 
     for k, got in enumerate((xrecv, yrecv, zrecv)):
         whole(k, got, hs_sem.at[k], hr_sem.at[k]).wait_recv()
 
     gate = [[jnp.where(h, 1.0, 0.0) for h in pair] for pair in has]
 
-    def split(value):
-        high = value.astype(bf16)
-        return high, (value - high.astype(f32)).astype(bf16)
-
     def diff(x):
-        return w_v[x] - f_v[x]
+        return w_v[x]
 
     for side, i in ((0, 0), (1, cells - 1)):
         r0, r1 = xrecv[side, 0] * gate[0][side], xrecv[side, 1] * gate[0][side]
@@ -304,8 +316,8 @@
     accc[:, SZ:2 * SZ] += out[2 * EX * PY:]
 
     even = lane % 2 == 0
-    dl = zrecv[0] * gate[2][0] - zsend[1]
-    dh = zrecv[1] * gate[2][1] - zsend[0]
+    dl = zrecv[0] * gate[2][0]
+    dh = zrecv[1] * gate[2][1]
     low = jnp.where(even, dl - 8.0 * pltpu.roll(dl, SZ - 1, 1), dl) * zd[0]
     high = jnp.where(even, -dh, 8.0 * pltpu.roll(dh, 1, 1) - dh) * zd[1]
     row, col = iota((QE + CQ, SY), 0), iota((QE + CQ, SY), 1)
@@ -323,10 +335,8 @@
     for p in range(CX):
         accc[p * CQ:(p + 1) * CQ, 2 * SZ:3 * SZ] += spread(2, 254 - 64 - 4 * p)
 
-    rows, cols = iota((SZ, 128), 0), iota((SZ, 128), 1)
-    bzc = weight(rows, cols % 4 + 4 * (cols // 16 - 1), SPC) * (SPC ** -1.5 / 24.0)
     stack = jnp.concatenate([accc[:, a * SZ:(a + 1) * SZ] for a in range(3)], axis=0)
-    shares = nn(stack, bzc)
+    shares = nn(stack, bzc_v[...])
     rows, cols = iota((CR, 128), 0), iota((CR, 128), 1)
     keep = ((cols // 4) % 4 == 2 * ((rows // CQ) % 2) + rows % 2) & (cols < 48)
     for f in range(3):
@@ -525,8 +535,9 @@
                 V((2, 2 * SX, SZ), f32), V((2, 2 * SX, SZ), f32), V((2, 2 * SX, SZ), f32),
                 V((2, SY, SZ), f32), V((2, SY, SZ), f32), V((2, SY, SZ), f32),
                 V((2, 5 * QE, KC), bf16), V((SX // SPF, 2, CR, KC), bf16),
-                V((2, EX * QE + CR, 4 * SX), bf16), V((4 * SX, 128), f32),
-                V((2, KC, 3 * SZ), bf16), V((2, KC, 3 * SZ), bf16),
+                V((2, EX * QE + CR, 4 * SX), bf16), V((4 * SX, 128), f32), V((SZ, 128), f32),
+                V((2 * SZ, 2 * SZ), bf16),
+                V((SX // SPF, KC, SZ), f32), V((2, 2, SY, SZ), f32),
                 V((2, EX, PY, 3 * SZ), f32), V((CR, 3 * SZ), f32),
                 V((2, 3, RZ, EX * PY), f32),
                 V((KX, KY, 128), f32), V((3, KX, KY, 128), f32),

time: 40.8 us -> 40.8 us (level)
  no operation moved by 1% of the time
where the time goes in v4:
time: 40.8 us; the launch traced here: 40.7 us
  Pallas kernels  38.7 us (95%)
  local copies, waits for them, and re-layouts  1.39 us (3%)
  between operations  0.64 us (2%)
    pallas_call x1, Pallas kernels, step(): pl.pallas_call(functools.partial(kernel, sizes), out_shape=(V(fine.shape,...  38.7 us
    unnamed x2, local copies, waits for them, and re-layouts  1.39 us

profile of v4, /device:TPU:1, one launch (start us, length us, event | category | flops | bytes accessed | tf_op | source)
XLA Modules:
  0.0 40.7 jit_solution(2582287524829680702)
XLA Ops:
  0.6 38.7 %shard_map.59 = (f32[3,8,8,16]{3,2,1,0:T(8,128)S(1)}, f32[3,16,16,32]{3,2,1,0:T(8,128)S(1)}) custom-call(f32[64,64,128]{2,1,0:T(8,128)} %w_hbm.1, f32[64,64,128]{2,1,0:T(8,128)} %f_hbm.1, f32[3,8,8,16]{3,2,1,0:T(8,128)} %fc_hbm.1, f32[3,16,16,32]{3,2,1,0:T(8,128)} %cc_hbm.1), custom_call_target="tpu_custom_call" | custom-call | tf_op jit(solution)/shard_map/pallas_call | solution.py:526
  39.3 0.6 %copy.8 = f32[3,8,8,16]{3,2,1,0:T(8,128)} copy(f32[3,8,8,16]{3,2,1,0:T(8,128)S(1)} %get-tuple-element.2) | data formatting | bytes 24576
  39.9 0.7 %copy.9 = f32[3,16,16,32]{3,2,1,0:T(8,128)} copy(f32[3,16,16,32]{3,2,1,0:T(8,128)S(1)} %get-tuple-element.3) | data formatting | bytes 196608

commit v5 on v4

--- a/solution.py
+++ b/solution.py
@@ -75,7 +75,7 @@
            w_v, f_v, fc_ref, cc_ref, s_v, xrecv, ysend, yrecv, yd, zsend, zrecv, zd,
            wf_v, wc_v, wy_v, wxe_v, bzc_v, pz_v, gz_v, zp_v,
            accf, accc, tz_v, clane, cbend, zmsg, zgot, a_v, agot, b_v, bgot,
-           cmsg, crecv, zrow, xrow, load_sem, small_sem, hs_sem, hr_sem,
+           cmsg, crecv, crest, xrow, load_sem, small_sem, hs_sem, hr_sem,
            ms_sem, mr_sem, n_sem, cs_sem, cr_sem):
     nx, ny, nz = sizes
     axes = ("gx", "gy", "gz")
@@ -106,7 +106,6 @@
         pltpu.make_async_copy(w_hbm.at[both], w_v.at[both], load_sem.at[c]).wait()
 
     has = [(me[k] > 0, me[k] < counts[k] - 1) for k in range(3)]
-    sides = [(d, e, f) for f in range(3) for d in range(3) for e in range(3)]
 
     def toward(step):
         return {axes[k]: lax.rem(me[k] + (counts[k] + step[k] - 1), counts[k])
@@ -123,17 +122,25 @@
     def far_first(n):
         return sorted(range(1, n), key=lambda d: -min(d, n - d))
 
+    columns = [(d, e) for d in range(3) for e in range(3)]
+    reach = [(n, dz) for dz in far_first(nz) + [0] for n in range(9) if (n, dz) != (4, 0)]
+
+    def column(n, dz):
+        there = toward(columns[n] + (1,))
+        if dz:
+            there[axes[2]] = lax.rem(me[2] + dz, nz)
+        return there
+
     barrier = pltpu.get_barrier_semaphore()
-    total = 0
-    for k, a in enumerate(axes):
-        for d in far_first(counts[k]):
+    for n, dz in reach:
+        pl.semaphore_signal(barrier, inc=1, device_id=column(n, dz), device_id_type=MESH)
+    total = len(reach)
+    for k in range(2):
+        for d in range(2, counts[k] - 1):
             pl.semaphore_signal(
-                barrier, inc=1, device_id={a: lax.rem(me[k] + d, counts[k])}, device_id_type=MESH
+                barrier, inc=1, device_id={axes[k]: lax.rem(me[k] + d, counts[k])},
+                device_id_type=MESH
             )
-            total += 1
-    for step in sides:
-        if sum(n != 1 for n in step) >= 2:
-            pl.semaphore_signal(barrier, inc=1, device_id=toward(step), device_id_type=MESH)
             total += 1
 
     zero_plane = jnp.zeros((2, SY, SZ), f32)
@@ -181,7 +188,7 @@
     pick = jnp.where(row == (col % 4 + SZ - 2) % SZ, 1.0, 0.0)
     pz_v[...] = jnp.where(col < SZ, slope, pick).astype(bf16)
     rows, cols = iota((SZ, 128), 0), iota((SZ, 128), 1)
-    bzc_v[...] = weight(rows, cols % 4 + 4 * (cols // 16 - 1), SPC) * (SPC ** -1.5 / 24.0)
+    bzc_v[...] = weight(rows, cols % 8 - 2, SPC) * (SPC ** -1.5 / 24.0)
     accf[...] = jnp.zeros(accf.shape, f32)
     accc[...] = jnp.zeros(accc.shape, f32)
 
@@ -338,27 +345,21 @@
     stack = jnp.concatenate([accc[:, a * SZ:(a + 1) * SZ] for a in range(3)], axis=0)
     shares = nn(stack, bzc_v[...])
     rows, cols = iota((CR, 128), 0), iota((CR, 128), 1)
-    keep = ((cols // 4) % 4 == 2 * ((rows // CQ) % 2) + rows % 2) & (cols < 48)
-    for f in range(3):
-        value = shares[0:CR]
-        value = value if f == 0 else pltpu.roll(value, 128 - 16 * f, 1)
-        for a in (1, 2):
-            moved = shares[a * CR:(a + 1) * CR]
-            moved = moved if a == f else pltpu.roll(moved, (128 + 16 * (a - f)) % 128, 1)
-            value = jnp.where(cols // 16 == a, moved, value)
-        value = jnp.where(keep, value, 0.0).reshape(3, 2, CQ, 128)
-        value = value[:, 0] + value[:, 1]
-        value = value + pltpu.roll(value, 7, 1)
-        for d in range(3):
-            for e in range(3):
-                cmsg[f * 9 + d * 3 + e] = value[d, 2 * e:2 * e + 1, :]
-
-    others = [n for n in range(27) if n != 13]
-    for n in sorted(others, key=lambda n: -sum(v != 1 for v in sides[n])):
+    keep = (cols // 32 == 2 * ((rows // CQ) % 2) + rows % 2) & (cols % 32 < 24)
+    value = jnp.where(cols % 32 < 8, shares[0:CR],
+                      jnp.where(cols % 32 < 16, shares[CR:2 * CR], shares[2 * CR:3 * CR]))
+    value = jnp.where(keep, value, 0.0).reshape(3, 2, CQ, 128)
+    value = value[:, 0] + value[:, 1]
+    value = value + pltpu.roll(value, 7, 1)
+    for n, (d, e) in enumerate(columns):
+        cmsg[n] = value[d, 2 * e:2 * e + 1, :]
+    mine = pl.ds(me[2], 1)
+    crecv[4, mine, :] = value[1, 2:3, :]
+    for n, dz in reach:
         pltpu.make_async_remote_copy(
-            src_ref=cmsg.at[n], dst_ref=crecv.at[others.index(26 - n)],
+            src_ref=cmsg.at[n], dst_ref=crecv.at[8 - n, mine, :],
             send_sem=n_sem.at[0], recv_sem=n_sem.at[1],
-            device_id=toward(sides[n]), device_id_type=MESH,
+            device_id=column(n, dz), device_id_type=MESH,
         ).start()
 
     rows, cols = iota((RZ, SZ), 0), iota((RZ, SZ), 1)
@@ -406,9 +407,7 @@
     def coarse_slot(k, n):
         if k == 0:
             return xrow.at[n]
-        if k == 1:
-            return xrow.at[me[0], :, pl.ds(n, 1), :]
-        return zrow.at[:, pl.ds(n, 1), :]
+        return xrow.at[me[0], :, pl.ds(n, 1), :]
 
     def coarse_start(k):
         for d in far_first(counts[k]):
@@ -420,23 +419,10 @@
 
     def coarse_whole(k):
         part = pl.ds(0, counts[k] - 1)
-        ref = (xrow.at[part], xrow.at[me[0], :, part, :], zrow.at[:, part, :])[k]
+        ref = (xrow.at[part], xrow.at[me[0], :, part, :])[k]
         return whole(k, ref, cs_sem.at[k], cr_sem.at[k])
 
     fine_start(2)
-
-    whole(0, crecv, n_sem.at[0], n_sem.at[1]).wait_recv()
-    own = cmsg[13]
-    for n in others:
-        own = own + jnp.where(inside(sides[n]), crecv[others.index(n)], 0.0)
-    at = iota((1, 128), 1)
-    own = pltpu.roll(own, 4 * me[2], 1)
-    for a in range(3):
-        value = own if a == 0 else pltpu.roll(own, 128 - 16 * a, 1)
-        for g in range(1, 4):
-            value = jnp.where(at // 32 == g, pltpu.roll(own, (128 + 28 * g - 16 * a) % 128, 1), value)
-        zrow[a, pl.ds(me[2], 1), :] = jnp.where((at % 32) // 4 == me[2], value, 0.0)
-    coarse_start(2)
 
     q_at, r_at = iota((KX, KY, 128), 1), iota((KX, KY, 128), 2)
 
@@ -453,9 +439,22 @@
         clane[:, :, 0:KZ] = cc_ref[a]
         cbend[a] = BEND * laplace(laplace(clane[...]))
 
-    coarse_whole(2).wait_recv()
+    all_shares = crest.at[pl.ds(0, len(reach))]
+    whole(0, all_shares, n_sem.at[0], n_sem.at[1]).wait_recv()
+    total = crecv[4]
+    for n, (d, e) in enumerate(columns):
+        if n != 4:
+            total = total + jnp.where(inside((d, e, 1)), crecv[n], 0.0)
+    sub, at = iota((nz, 128), 0), iota((nz, 128), 1) % 32
+    keep = (at >= 4 * sub - 2) & (at < 4 * sub + 6) & (at < KZ)
     for a in range(3):
-        xrow[me[0], a, pl.ds(me[1], 1), :] = jnp.sum(zrow[a], axis=0, keepdims=True)
+        value = None
+        for n in range(nz):
+            shift = (4 * n - 2 - 8 * a) % 128
+            moved = pltpu.roll(total, shift, 1) if shift else total
+            value = moved if n == 0 else jnp.where(sub == n, moved, value)
+        xrow[me[0], a, pl.ds(me[1], 1), :] = jnp.sum(
+            jnp.where(keep, value, 0.0), axis=0, keepdims=True)
     coarse_start(1)
 
     fine_whole(2).wait_recv()
@@ -495,8 +494,9 @@
     for k, got in enumerate((xrecv, yrecv, zrecv)):
         whole(k, got, hs_sem.at[k], hr_sem.at[k]).wait_send()
         fine_whole(k).wait_send()
-        coarse_whole(k).wait_send()
-    whole(0, crecv, n_sem.at[0], n_sem.at[1]).wait_send()
+        if k < 2:
+            coarse_whole(k).wait_send()
+    whole(0, all_shares, n_sem.at[0], n_sem.at[1]).wait_send()
 
     coarse_whole(0).wait_recv()
     for i in range(nx):
@@ -544,10 +544,10 @@
                 V((2, 2, 8, EX * PY), f32), V((2, 2, 8, EX * PY), f32),
                 V((2, 3 * PZ, EX * PY), f32), V((2, 3 * PZ, EX * PY), f32),
                 V((3 * PZ, EX * PY), f32), V((2, 3 * PZ, EX * PY), f32),
-                V((27, 1, 128), f32), V((26, 1, 128), f32),
-                V((3, sizes[2], 128), f32), V((sizes[0], 3, sizes[1], 128), f32),
+                V((9, 1, 128), f32), V((9, sizes[2], 128), f32),
+                V((9 * sizes[2], 128), f32), V((sizes[0], 3, sizes[1], 128), f32),
                 D((SX // SPF,)), D((2,)), D((3,)), D((3,)),
-                D((3,)), D((3,)), D((2,)), D((3,)), D((3,)),
+                D((3,)), D((3,)), D((2,)), D((2,)), D((2,)),
             ],
             compiler_params=pltpu.CompilerParams(
                 collective_id=0, has_side_effects=True, vmem_limit_bytes=66000000

time: 40.8 us -> 38.2 us (0.936)
  Pallas kernels: 38.7 us -> 36.1 us
    pallas_call x1, Pallas kernels: 38.7 us -> 36.1 us  [step(): pl.pallas_call(functools.partial(kernel, sizes), out_shape=(V(fine.shape,...]
where the time goes in v5:
time: 38.2 us; the launch traced here: 38.1 us
  Pallas kernels  36.1 us (95%)
  local copies, waits for them, and re-layouts  1.39 us (4%)
  between operations  0.64 us (2%)
    pallas_call x1, Pallas kernels, step(): pl.pallas_call(functools.partial(kernel, sizes), out_shape=(V(fine.shape,...  36.1 us
    unnamed x2, local copies, waits for them, and re-layouts  1.39 us

profile of v5, /device:TPU:1, one launch (start us, length us, event | category | flops | bytes accessed | tf_op | source)
XLA Modules:
  0.0 38.1 jit_solution(849645383799452574)
XLA Ops:
  0.6 36.1 %shard_map.59 = (f32[3,8,8,16]{3,2,1,0:T(8,128)S(1)}, f32[3,16,16,32]{3,2,1,0:T(8,128)S(1)}) custom-call(f32[64,64,128]{2,1,0:T(8,128)} %w_hbm.1, f32[64,64,128]{2,1,0:T(8,128)} %f_hbm.1, f32[3,8,8,16]{3,2,1,0:T(8,128)} %fc_hbm.1, f32[3,16,16,32]{3,2,1,0:T(8,128)} %cc_hbm.1), custom_call_target="tpu_custom_call" | custom-call | tf_op jit(solution)/shard_map/pallas_call | solution.py:526
  36.7 0.6 %copy.8 = f32[3,8,8,16]{3,2,1,0:T(8,128)} copy(f32[3,8,8,16]{3,2,1,0:T(8,128)S(1)} %get-tuple-element.2) | data formatting | bytes 24576
  37.4 0.7 %copy.9 = f32[3,16,16,32]{3,2,1,0:T(8,128)} copy(f32[3,16,16,32]{3,2,1,0:T(8,128)S(1)} %get-tuple-element.3) | data formatting | bytes 196608

commit v6 on v5

--- a/solution.py
+++ b/solution.py
@@ -76,7 +76,7 @@
            wf_v, wc_v, wy_v, wxe_v, bzc_v, pz_v, gz_v, zp_v,
            accf, accc, tz_v, clane, cbend, zmsg, zgot, a_v, agot, b_v, bgot,
            cmsg, crecv, crest, xrow, load_sem, small_sem, hs_sem, hr_sem,
-           ms_sem, mr_sem, n_sem, cs_sem, cr_sem):
+           ms_sem, mr_sem, n_sem, cs_sem, cr_sem, ready):
     nx, ny, nz = sizes
     axes = ("gx", "gy", "gz")
     counts = sizes
@@ -132,15 +132,18 @@
         return there
 
     barrier = pltpu.get_barrier_semaphore()
-    for n, dz in reach:
-        pl.semaphore_signal(barrier, inc=1, device_id=column(n, dz), device_id_type=MESH)
-    total = len(reach)
-    for k in range(2):
-        for d in range(2, counts[k] - 1):
+    total = 0
+    for k in (2, 1, 0):
+        for d in far_first(counts[k]):
             pl.semaphore_signal(
                 barrier, inc=1, device_id={axes[k]: lax.rem(me[k] + d, counts[k])},
                 device_id_type=MESH
             )
+            total += 1
+    around = [n for n in range(9) if n != 4]
+    for n in around:
+        if n % 2 == 0:
+            pl.semaphore_signal(barrier, inc=1, device_id=column(n, 0), device_id_type=MESH)
             total += 1
 
     zero_plane = jnp.zeros((2, SY, SZ), f32)
@@ -150,48 +153,12 @@
     s_v[2:SX + 2, 6:8, :] = zero_rows
     s_v[2:SX + 2, 8 + SY:10 + SY, :] = zero_rows
 
-    def split_store(ref, index, value):
-        high = value.astype(bf16)
-        ref[index + (0,)] = high
-        ref[index + (1,)] = (value - high.astype(f32)).astype(bf16)
-
-    def ext_q(q):
-        return jnp.where(q < PY, q, jnp.where(q < PY + 2, q - PY - 2, q - 2))
-
-    def outer(along_x, along_y):
-        return jnp.concatenate([along_x[p:p + 1] * along_y for p in range(along_x.shape[0])], axis=0)
-
-    col = iota((8, KC), 1)
-    col2 = iota((QE, KC), 1)
-    split_store(wf_v, (), outer(weight(col // SY, iota((8, KC), 0) - 2, SPF)[0:5],
-                                weight(col2 % SY, ext_q(iota((QE, KC), 0)), SPF)))
-    along_y = weight(col % SY, iota((8, KC), 0) - 2, SPC)
-    for c in range(cells):
-        split_store(wc_v, (c,), outer(
-            weight(col // SY + c * SPF, iota((8, KC), 0) - 2, SPC)[0:CX], along_y))
-    col, row = iota((QE, 4 * SX), 1), iota((QE, 4 * SX), 0)
-    face_x, face_y = (col % (2 * SX)) // 2, col % 2 + (SY - 2) * (col // (2 * SX))
-    along_x = weight(face_x, row - 2, SPF)[0:EX]
-    along_y = weight(face_y, ext_q(row), SPF)
-    split_store(wy_v, (), jnp.concatenate([
-        outer(along_x, along_y[0:PY]), outer(along_x, along_y[PY:QE]),
-        outer(weight(face_x, row - 2, SPC)[0:CX], weight(face_y, row - 2, SPC)[0:CQ])], axis=0))
-    row, col = iota((4 * SX, 128), 0), iota((4 * SX, 128), 1)
-    face_x = (row % (2 * SX)) // 4 + jnp.where(row % 4 < 2, SX // 2, 0)
-    place = row % 2 + 2 - 2 * (row // (2 * SX))
-    wxe_v[...] = jnp.where(col % 4 == place, jnp.where(
-        col < 64, weight(face_x, col // 4 - 2, SPF), weight(face_x, col // 4 - 18, SPC)), 0.0)
     row, col = iota((2 * SZ, 2 * SZ), 0) % SZ, iota((2 * SZ, 2 * SZ), 1)
     away = row - col
     slope = jnp.where(away == 1, 8.0, jnp.where(away == -1, -8.0, jnp.where(
         away == -2, 1.0, jnp.where(away == 2, -1.0, 0.0))))
     pick = jnp.where(row == (col % 4 + SZ - 2) % SZ, 1.0, 0.0)
     pz_v[...] = jnp.where(col < SZ, slope, pick).astype(bf16)
-    rows, cols = iota((SZ, 128), 0), iota((SZ, 128), 1)
-    bzc_v[...] = weight(rows, cols % 8 - 2, SPC) * (SPC ** -1.5 / 24.0)
-    accf[...] = jnp.zeros(accf.shape, f32)
-    accc[...] = jnp.zeros(accc.shape, f32)
-
     lane = iota((SY, SZ), 1)
     half_x = SX // 2
 
@@ -230,6 +197,8 @@
         ref[1] = jnp.where(upper, pltpu.roll(zp_v[n, 0], 2, 1), zp_v[n, 1])
 
     pl.semaphore_wait(barrier, total)
+    for n in around:
+        pl.semaphore_signal(ready, inc=1, device_id=column(n, 0), device_id_type=MESH)
 
     def neighbour_copy(k, side, src, dst, send, recv):
         step = [1, 1, 1]
@@ -253,6 +222,42 @@
     for k in (1, 2, 0):
         for side in range(2):
             halo(k, side).start()
+
+    def split_store(ref, index, value):
+        high = value.astype(bf16)
+        ref[index + (0,)] = high
+        ref[index + (1,)] = (value - high.astype(f32)).astype(bf16)
+
+    def ext_q(q):
+        return jnp.where(q < PY, q, jnp.where(q < PY + 2, q - PY - 2, q - 2))
+
+    def outer(along_x, along_y):
+        return jnp.concatenate([along_x[p:p + 1] * along_y for p in range(along_x.shape[0])], axis=0)
+
+    col = iota((8, KC), 1)
+    col2 = iota((QE, KC), 1)
+    split_store(wf_v, (), outer(weight(col // SY, iota((8, KC), 0) - 2, SPF)[0:5],
+                                weight(col2 % SY, ext_q(iota((QE, KC), 0)), SPF)))
+    along_y = weight(col % SY, iota((8, KC), 0) - 2, SPC)
+    for c in range(cells):
+        split_store(wc_v, (c,), outer(
+            weight(col // SY + c * SPF, iota((8, KC), 0) - 2, SPC)[0:CX], along_y))
+    col, row = iota((QE, 4 * SX), 1), iota((QE, 4 * SX), 0)
+    face_x, face_y = (col % (2 * SX)) // 2, col % 2 + (SY - 2) * (col // (2 * SX))
+    along_x = weight(face_x, row - 2, SPF)[0:EX]
+    along_y = weight(face_y, ext_q(row), SPF)
+    split_store(wy_v, (), jnp.concatenate([
+        outer(along_x, along_y[0:PY]), outer(along_x, along_y[PY:QE]),
+        outer(weight(face_x, row - 2, SPC)[0:CX], weight(face_y, row - 2, SPC)[0:CQ])], axis=0))
+    row, col = iota((4 * SX, 128), 0), iota((4 * SX, 128), 1)
+    face_x = (row % (2 * SX)) // 4 + jnp.where(row % 4 < 2, SX // 2, 0)
+    place = row % 2 + 2 - 2 * (row // (2 * SX))
+    wxe_v[...] = jnp.where(col % 4 == place, jnp.where(
+        col < 64, weight(face_x, col // 4 - 2, SPF), weight(face_x, col // 4 - 18, SPC)), 0.0)
+    rows, cols = iota((SZ, 128), 0), iota((SZ, 128), 1)
+    bzc_v[...] = weight(rows, cols % 8 - 2, SPC) * (SPC ** -1.5 / 24.0)
+    accf[...] = jnp.zeros(accf.shape, f32)
+    accc[...] = jnp.zeros(accc.shape, f32)
 
     def forces(i):
         T = 16
@@ -355,6 +360,7 @@
         cmsg[n] = value[d, 2 * e:2 * e + 1, :]
     mine = pl.ds(me[2], 1)
     crecv[4, mine, :] = value[1, 2:3, :]
+    pl.semaphore_wait(ready, len(around))
     for n, dz in reach:
         pltpu.make_async_remote_copy(
             src_ref=cmsg.at[n], dst_ref=crecv.at[8 - n, mine, :],
@@ -547,7 +553,7 @@
                 V((9, 1, 128), f32), V((9, sizes[2], 128), f32),
                 V((9 * sizes[2], 128), f32), V((sizes[0], 3, sizes[1], 128), f32),
                 D((SX // SPF,)), D((2,)), D((3,)), D((3,)),
-                D((3,)), D((3,)), D((2,)), D((2,)), D((2,)),
+                D((3,)), D((3,)), D((2,)), D((2,)), D((2,)), pltpu.SemaphoreType.REGULAR,
             ],
             compiler_params=pltpu.CompilerParams(
                 collective_id=0, has_side_effects=True, vmem_limit_bytes=66000000

time: 38.2 us -> 36.8 us (0.963)
  Pallas kernels: 36.1 us -> 34.7 us
    pallas_call x1, Pallas kernels: 36.1 us -> 34.7 us  [step(): pl.pallas_call(functools.partial(kernel, sizes), out_shape=(V(fine.shape,...]
where the time goes in v6:
time: 36.8 us; the launch traced here: 36.7 us
  Pallas kernels  34.7 us (94%)
  local copies, waits for them, and re-layouts  1.39 us (4%)
  between operations  0.64 us (2%)
    pallas_call x1, Pallas kernels, step(): pl.pallas_call(functools.partial(kernel, sizes), out_shape=(V(fine.shape,...  34.7 us
    unnamed x2, local copies, waits for them, and re-layouts  1.39 us

profile of v6, /device:TPU:1, one launch (start us, length us, event | category | flops | bytes accessed | tf_op | source)
XLA Modules:
  0.0 36.7 jit_solution(11744748595956873526)
XLA Ops:
  0.6 34.7 %shard_map.59 = (f32[3,8,8,16]{3,2,1,0:T(8,128)S(1)}, f32[3,16,16,32]{3,2,1,0:T(8,128)S(1)}) custom-call(f32[64,64,128]{2,1,0:T(8,128)} %w_hbm.1, f32[64,64,128]{2,1,0:T(8,128)} %f_hbm.1, f32[3,8,8,16]{3,2,1,0:T(8,128)} %fc_hbm.1, f32[3,16,16,32]{3,2,1,0:T(8,128)} %cc_hbm.1), custom_call_target="tpu_custom_call" | custom-call | tf_op jit(solution)/shard_map/pallas_call | solution.py:532
  35.3 0.6 %copy.8 = f32[3,8,8,16]{3,2,1,0:T(8,128)} copy(f32[3,8,8,16]{3,2,1,0:T(8,128)S(1)} %get-tuple-element.2) | data formatting | bytes 24576
  35.9 0.7 %copy.9 = f32[3,16,16,32]{3,2,1,0:T(8,128)} copy(f32[3,16,16,32]{3,2,1,0:T(8,128)S(1)} %get-tuple-element.3) | data formatting | bytes 196608

commit v7 on v5

--- a/solution.py
+++ b/solution.py
@@ -76,7 +76,7 @@
            wf_v, wc_v, wy_v, wxe_v, bzc_v, pz_v, gz_v, zp_v,
            accf, accc, tz_v, clane, cbend, zmsg, zgot, a_v, agot, b_v, bgot,
            cmsg, crecv, crest, xrow, load_sem, small_sem, hs_sem, hr_sem,
-           ms_sem, mr_sem, n_sem, cs_sem, cr_sem):
+           ms_sem, mr_sem, n_sem, cs_sem, cr_sem, ready):
     nx, ny, nz = sizes
     axes = ("gx", "gy", "gz")
     counts = sizes
@@ -132,15 +132,18 @@
         return there
 
     barrier = pltpu.get_barrier_semaphore()
-    for n, dz in reach:
-        pl.semaphore_signal(barrier, inc=1, device_id=column(n, dz), device_id_type=MESH)
-    total = len(reach)
-    for k in range(2):
-        for d in range(2, counts[k] - 1):
+    total = 0
+    for k in (2, 1, 0):
+        for d in far_first(counts[k]):
             pl.semaphore_signal(
                 barrier, inc=1, device_id={axes[k]: lax.rem(me[k] + d, counts[k])},
                 device_id_type=MESH
             )
+            total += 1
+    around = [n for n in range(9) if n != 4]
+    for n in around:
+        if n % 2 == 0:
+            pl.semaphore_signal(barrier, inc=1, device_id=column(n, 0), device_id_type=MESH)
             total += 1
 
     zero_plane = jnp.zeros((2, SY, SZ), f32)
@@ -150,6 +153,12 @@
     s_v[2:SX + 2, 6:8, :] = zero_rows
     s_v[2:SX + 2, 8 + SY:10 + SY, :] = zero_rows
 
+    row, col = iota((2 * SZ, 2 * SZ), 0) % SZ, iota((2 * SZ, 2 * SZ), 1)
+    away = row - col
+    slope = jnp.where(away == 1, 8.0, jnp.where(away == -1, -8.0, jnp.where(
+        away == -2, 1.0, jnp.where(away == 2, -1.0, 0.0))))
+    pick = jnp.where(row == (col % 4 + SZ - 2) % SZ, 1.0, 0.0)
+    pz_v[...] = jnp.where(col < SZ, slope, pick).astype(bf16)
     def split_store(ref, index, value):
         high = value.astype(bf16)
         ref[index + (0,)] = high
@@ -181,12 +190,6 @@
     place = row % 2 + 2 - 2 * (row // (2 * SX))
     wxe_v[...] = jnp.where(col % 4 == place, jnp.where(
         col < 64, weight(face_x, col // 4 - 2, SPF), weight(face_x, col // 4 - 18, SPC)), 0.0)
-    row, col = iota((2 * SZ, 2 * SZ), 0) % SZ, iota((2 * SZ, 2 * SZ), 1)
-    away = row - col
-    slope = jnp.where(away == 1, 8.0, jnp.where(away == -1, -8.0, jnp.where(
-        away == -2, 1.0, jnp.where(away == 2, -1.0, 0.0))))
-    pick = jnp.where(row == (col % 4 + SZ - 2) % SZ, 1.0, 0.0)
-    pz_v[...] = jnp.where(col < SZ, slope, pick).astype(bf16)
     rows, cols = iota((SZ, 128), 0), iota((SZ, 128), 1)
     bzc_v[...] = weight(rows, cols % 8 - 2, SPC) * (SPC ** -1.5 / 24.0)
     accf[...] = jnp.zeros(accf.shape, f32)
@@ -199,17 +202,24 @@
         high = value.astype(bf16)
         return high, (value - high.astype(f32)).astype(bf16)
 
-    for c in range(cells):
-        load_wait(c)
+    def face_rows(c):
+        for x in range(c * SPF, (c + 1) * SPF):
+            for side, part in ((0, slice(0, 8)), (1, slice(SY - 8, SY))):
+                w, f = w_v[x, part, :], f_v[x, part, :]
+                rows = slice(6 * side, 6 * side + 2)
+                ysend[side, 2 * x:2 * x + 2, :] = (w + f)[rows]
+                yd[side, 2 * x:2 * x + 2, :] = (w - f)[rows]
+
+    outer_planes = (0, 1, SX - 2, SX - 1)
+
+    def sums(c):
         wide = ([], [])
         for x in range(c * SPF, (c + 1) * SPF):
             w, f = w_v[x], f_v[x]
             s, d = w + f, w - f
-            s_v[x + 2, 8:8 + SY, :] = s
+            if x not in outer_planes:
+                s_v[x + 2, 8:8 + SY, :] = s
             w_v[x] = d
-            for side, part in ((0, slice(0, 2)), (1, slice(SY - 2, SY))):
-                ysend[side, 2 * x:2 * x + 2, :] = s[part]
-                yd[side, 2 * x:2 * x + 2, :] = d[part]
             for n, value in enumerate((s, d)):
                 wide[n].append(jnp.concatenate(split(value), axis=1))
         out = jnp.dot(jnp.concatenate(wide[0], axis=0), pz_v[...], preferred_element_type=f32)
@@ -224,12 +234,19 @@
                 here = lane // 4 == (c * SPF + xx) % half_x
                 pack = value if pack is None else jnp.where(here, value, pack)
             zp_v[n, tile] = pack
-    upper = lane % 4 >= 2
-    for n, ref in enumerate((zsend, zd)):
-        ref[0] = jnp.where(upper, zp_v[n, 0], pltpu.roll(zp_v[n, 1], SZ - 2, 1))
-        ref[1] = jnp.where(upper, pltpu.roll(zp_v[n, 0], 2, 1), zp_v[n, 1])
+    half = cells // 2
+    for c in range(cells):
+        load_wait(c)
+        face_rows(c)
+        for x in outer_planes:
+            if x // SPF == c:
+                s_v[x + 2, 8:8 + SY, :] = w_v[x] + f_v[x]
+        if c < half:
+            sums(c)
 
     pl.semaphore_wait(barrier, total)
+    for n in around:
+        pl.semaphore_signal(ready, inc=1, device_id=column(n, 0), device_id_type=MESH)
 
     def neighbour_copy(k, side, src, dst, send, recv):
         step = [1, 1, 1]
@@ -250,9 +267,19 @@
     def whole(k, ref, send, recv):
         return neighbour_copy(k, 0, ref, ref, send, recv)
 
-    for k in (1, 2, 0):
+    for k in (1, 0):
         for side in range(2):
             halo(k, side).start()
+
+    for c in range(half, cells):
+        sums(c)
+    upper = lane % 4 >= 2
+    for n, ref in enumerate((zsend, zd)):
+        ref[0] = jnp.where(upper, zp_v[n, 0], pltpu.roll(zp_v[n, 1], SZ - 2, 1))
+        ref[1] = jnp.where(upper, pltpu.roll(zp_v[n, 0], 2, 1), zp_v[n, 1])
+
+    for side in range(2):
+        halo(2, side).start()
 
     def forces(i):
         T = 16
@@ -355,6 +382,7 @@
         cmsg[n] = value[d, 2 * e:2 * e + 1, :]
     mine = pl.ds(me[2], 1)
     crecv[4, mine, :] = value[1, 2:3, :]
+    pl.semaphore_wait(ready, len(around))
     for n, dz in reach:
         pltpu.make_async_remote_copy(
             src_ref=cmsg.at[n], dst_ref=crecv.at[8 - n, mine, :],
@@ -547,7 +575,7 @@
                 V((9, 1, 128), f32), V((9, sizes[2], 128), f32),
                 V((9 * sizes[2], 128), f32), V((sizes[0], 3, sizes[1], 128), f32),
                 D((SX // SPF,)), D((2,)), D((3,)), D((3,)),
-                D((3,)), D((3,)), D((2,)), D((2,)), D((2,)),
+                D((3,)), D((3,)), D((2,)), D((2,)), D((2,)), pltpu.SemaphoreType.REGULAR,
             ],
             compiler_params=pltpu.CompilerParams(
                 collective_id=0, has_side_effects=True, vmem_limit_bytes=66000000

time: 38.2 us -> 36.7 us (0.961)
  Pallas kernels: 36.1 us -> 34.6 us
    pallas_call x1, Pallas kernels: 36.1 us -> 34.6 us  [step(): pl.pallas_call(functools.partial(kernel, sizes), out_shape=(V(fine.shape,...]
where the time goes in v7:
time: 36.7 us; the launch traced here: 36.6 us
  Pallas kernels  34.6 us (94%)
  local copies, waits for them, and re-layouts  1.39 us (4%)
  between operations  0.64 us (2%)
    pallas_call x1, Pallas kernels, step(): pl.pallas_call(functools.partial(kernel, sizes), out_shape=(V(fine.shape,...  34.6 us
    unnamed x2, local copies, waits for them, and re-layouts  1.39 us

profile of v7, /device:TPU:1, one launch (start us, length us, event | category | flops | bytes accessed | tf_op | source)
XLA Modules:
  0.0 36.6 jit_solution(13651486528523153146)
XLA Ops:
  0.6 34.6 %shard_map.59 = (f32[3,8,8,16]{3,2,1,0:T(8,128)S(1)}, f32[3,16,16,32]{3,2,1,0:T(8,128)S(1)}) custom-call(f32[64,64,128]{2,1,0:T(8,128)} %w_hbm.1, f32[64,64,128]{2,1,0:T(8,128)} %f_hbm.1, f32[3,8,8,16]{3,2,1,0:T(8,128)} %fc_hbm.1, f32[3,16,16,32]{3,2,1,0:T(8,128)} %cc_hbm.1), custom_call_target="tpu_custom_call" | custom-call | tf_op jit(solution)/shard_map/pallas_call | solution.py:554
  35.2 0.6 %copy.8 = f32[3,8,8,16]{3,2,1,0:T(8,128)} copy(f32[3,8,8,16]{3,2,1,0:T(8,128)S(1)} %get-tuple-element.2) | data formatting | bytes 24576
  35.9 0.7 %copy.9 = f32[3,16,16,32]{3,2,1,0:T(8,128)} copy(f32[3,16,16,32]{3,2,1,0:T(8,128)S(1)} %get-tuple-element.3) | data formatting | bytes 196608

commit v8 on v7

--- a/solution.py
+++ b/solution.py
@@ -495,9 +495,6 @@
             a_v[half, a * PZ:(a + 1) * PZ, :] = tz_v[half, a, 0:PZ, :]
     fine_start(1)
 
-    coarse_whole(1).wait_recv()
-    coarse_start(0)
-
     fine_whole(1).wait_recv()
     shape = (EX * PY, EX * PY)
     rows, cols = iota(shape, 0), iota(shape, 1)
@@ -507,6 +504,9 @@
     high = jnp.where(p_same & (q == r - (PY - 2)) & (r >= PY - 2), 1.0, 0.0)
     b_v[...] = (a_v[0] + nn(agot[0] * gate[1][0], low) + nn(agot[1] * gate[1][1], high))
     fine_start(0)
+
+    coarse_whole(1).wait_recv()
+    coarse_start(0)
 
     fine_whole(0).wait_recv()
     shape = (PX * PY, EX * PY)

time: 36.7 us -> 36.7 us (level)
  no operation moved by 1% of the time
where the time goes in v8:
time: 36.7 us; the launch traced here: 36.6 us
  Pallas kernels  34.6 us (94%)
  local copies, waits for them, and re-layouts  1.39 us (4%)
  between operations  0.64 us (2%)
    pallas_call x1, Pallas kernels, step(): pl.pallas_call(functools.partial(kernel, sizes), out_shape=(V(fine.shape,...  34.6 us
    unnamed x2, local copies, waits for them, and re-layouts  1.39 us

profile of v8, /device:TPU:1, one launch (start us, length us, event | category | flops | bytes accessed | tf_op | source)
XLA Modules:
  0.0 36.6 jit_solution(9515189241045448704)
XLA Ops:
  0.6 34.6 %shard_map.59 = (f32[3,8,8,16]{3,2,1,0:T(8,128)S(1)}, f32[3,16,16,32]{3,2,1,0:T(8,128)S(1)}) custom-call(f32[64,64,128]{2,1,0:T(8,128)} %w_hbm.1, f32[64,64,128]{2,1,0:T(8,128)} %f_hbm.1, f32[3,8,8,16]{3,2,1,0:T(8,128)} %fc_hbm.1, f32[3,16,16,32]{3,2,1,0:T(8,128)} %cc_hbm.1), custom_call_target="tpu_custom_call" | custom-call | tf_op jit(solution)/shard_map/pallas_call | solution.py:554
  35.2 0.6 %copy.8 = f32[3,8,8,16]{3,2,1,0:T(8,128)} copy(f32[3,8,8,16]{3,2,1,0:T(8,128)S(1)} %get-tuple-element.2) | data formatting | bytes 24576
  35.9 0.7 %copy.9 = f32[3,16,16,32]{3,2,1,0:T(8,128)} copy(f32[3,16,16,32]{3,2,1,0:T(8,128)S(1)} %get-tuple-element.3) | data formatting | bytes 196608
